TPU v7x, 32 devices: a whole 2x2x4 slice. The times are simulated.
32 devices in a mesh: sky: 8 (over z, y), band: 4 (over x, core).
Axes of the slice: x: 2, y: 2, z: 4, core: 2. Of those that a mesh axis runs over, the one named last changes fastest.
Arguments:
- magnitudes: float32 [4, 8, 16384], P('band', None, 'sky'), may hold values from -7 to 7
- weights: float32 [4, 8, 16384], P('band', None, 'sky'), may hold values from 0.25 to 4
- slots: int32 [4, 8, 16384], P('band', None, 'sky'), may hold values from 0 to 31, as said below
- block_fields: int32 [64, 32], P('sky'), may hold values from 0 to 4096, as said below
- owner: int32 [4096], replicated, may hold values from 0 to 7, as said below
- colors: int32 [4096], replicated, may hold values from 0 to 7
- color_terms: float32 [4, 4], replicated, may hold values from -0.25 to 0.25
Outputs:
- zero_points: float32 [4, 4096], P('band', 'sky')
- star_mags: float32 [4, 16384], P('band', 'sky')
- misfit: float32 [4, 4], P(None, 'band')
Inputs may be any that keep to these rules, and one draw needn't show every extreme that they name: `block_fields`: the live entries of each list come first, are distinct, and name fields owned by the block's own sky tile or by the tiles one index below or above it, cyclically over 8 tiles; the remaining entries equal 4096. A list holds 16 or more live entries, and every tile has a block with all 32 live. `owner`: each sky tile owns exactly 512 fields. `slots`: each observation names a live entry of its block's list.
All inputs are finite; a program needn't handle non-finite values.
Results may differ from a plain program's by a relative error of at most 0.00023.
Values sent between devices are 32-bit elements; how exact they have to be, the bound alone decides.
No kernel may reach another device: no remote copies, remote signals or barrier semaphores. Data moves between devices by JAX's collectives and lax.ppermute only.
A program may use at most 64 MiB of HBM per device.

v0:
```python
import functools

import jax
import jax.numpy as jnp
from jax import lax
from jax.experimental import pallas as pl
from jax.experimental.pallas import tpu as pltpu
from jax.sharding import PartitionSpec as P


COLORS = 8
SWEEPS = 4


PRIOR_WEIGHT = 1.0
LANES = 128
SUBS = 8
HALF = LANES // 2
FOLDS = (2, 3)
MOST = max(FOLDS) ** 2
F32 = jnp.float32
BF16 = jnp.bfloat16
I32 = jnp.int32
NT = (((1,), (1,)), ((), ()))
NN = (((1,), (0,)), ((), ()))


def iota(shape, axis):
    return lax.broadcasted_iota(I32, shape, axis)


def pick(table, idx):
    return jnp.take_along_axis(table, idx, axis=1, mode="promise_in_bounds")


def row_to(value, rows):
    return jnp.broadcast_to(value, (rows, value.shape[1]))


def table_lookup(table_ref, ids, rows, init):
    out = jnp.full(ids.shape, init, F32)
    for r in range(rows):
        hit = pick(row_to(table_ref[r : r + 1, :], ids.shape[0]), ids & (LANES - 1))
        out = jnp.where((ids >> 7) == r, hit, out)
    return out


def mixing_row(terms_ref, mine, bands):
    total = terms_ref[mine, 0]
    for b in range(1, bands):
        total = total + terms_ref[mine, b]
    return [terms_ref[mine, b] + jnp.where(mine == b, 1.0 - total, 0.0) for b in range(bands)]


def pack_kernel(mag_ref, wt_ref, slot_ref, out_ref):
    obs, stars = mag_ref.shape
    w = wt_ref[...]
    out_ref[0:obs, 0:stars] = w
    out_ref[obs : 2 * obs, 0:stars] = slot_ref[...].astype(F32)
    base = jnp.sum(w * mag_ref[...], axis=0, keepdims=True) / jnp.sum(w, axis=0, keepdims=True)
    for i in range(stars // LANES):
        out_ref[i : i + 1, stars : stars + LANES] = base[:, i * LANES : (i + 1) * LANES]


def tile_kernel(
    dims, terms_ref, raw_ref, mag_ref, lists_ref, colors_ref, out0_ref, out1_ref, tab_ref, pad_ref, sq_ref, wf_ref, x_ref, colf_ref
):
    bands, obs, stars, blocks, entries, fields, blk_rows = dims
    lane = iota((SUBS, LANES), 1)
    pad_ref[...] = jnp.full((SUBS, LANES), fields, I32)
    pad_ref[:, :entries] = lists_ref[...]
    ids = pad_ref[...]
    live = ids < fields
    safe = jnp.where(live, ids, 0)
    colf_ref[...] = colors_ref[...].astype(F32)
    color = table_lookup(colf_ref, safe, fields // LANES, 0.0).astype(I32)
    key = jnp.where(live, color * entries + lane, COLORS * entries)
    rank = jnp.zeros((SUBS, LANES), I32)
    for e in range(entries):
        rank = rank + jnp.where(key[:, e : e + 1] < key, 1, 0)
    live_f = jnp.where(live, 1.0, 0.0)
    dead = entries - jnp.sum(live_f, axis=1, keepdims=True).astype(I32)
    pos = jnp.where(live, rank + ((dead * color) >> (COLORS.bit_length() - 1)), 4 * LANES)
    inv = jnp.full((SUBS, LANES), -1, I32)
    for e in range(entries):
        inv = jnp.where(pos[:, e : e + 1] == lane, e, inv)
    used = inv >= 0
    inv_safe = jnp.where(used, inv, 0)
    fpos = jnp.where(used, pick(ids, inv_safe).astype(F32), -1.0)
    cpos = jnp.where(used, pick(color, inv_safe).astype(F32), float(COLORS))
    pos_live = jnp.where(live, pos, 0)
    tab_ref[...] = ((pos_live >> 1) & 1) * HALF + (pos_live >> 2) * (2 * bands) + (pos_live & 1) * bands

    sq_ref[...] = jnp.zeros((LANES, LANES), F32)
    sq_ref[0:SUBS, :] = inv.astype(F32)
    inv_t = sq_ref[...].T
    mine = lax.axis_index("band")
    mix_ref = mixing_row(terms_ref, mine, bands)
    lanes_sq = iota((entries, LANES), 1)
    t0_cols = jnp.zeros((entries, LANES), F32)
    wt_cols = jnp.zeros((entries, LANES), F32)
    for blk in range(blocks):
        lo, hi = blk * blk_rows, (blk + 1) * blk_rows
        inv_col = jnp.broadcast_to(inv_t[0:entries, blk : blk + 1], (entries, blk_rows))
        pred = jnp.zeros((1, blk_rows), F32)
        for b in range(bands):
            w = raw_ref[b, 0:obs, lo:hi]
            slot = raw_ref[b, obs : 2 * obs, lo:hi]
            acc = jnp.zeros((entries, blk_rows), F32)
            for k in range(obs):
                acc = acc + jnp.where(slot[k : k + 1] == inv_col, w[k : k + 1], 0.0)
            scale = mix_ref[b] / jnp.sum(w, axis=0, keepdims=True)
            wf_ref[b * entries : (b + 1) * entries, :] = acc
            x_ref[b * entries : (b + 1) * entries, :] = acc * scale
            pieces = blk_rows // LANES
            means = raw_ref[b, blk * pieces : (blk + 1) * pieces, stars : stars + LANES]
            pred = pred + mix_ref[b] * jnp.concatenate([means[i : i + 1] for i in range(pieces)], axis=1)
        own = wf_ref[pl.ds(mine * entries, entries), :]
        gram = lax.dot_general(own, x_ref[...], NT, precision=lax.Precision.HIGHEST, preferred_element_type=F32)
        cut = entries // 2
        out0_ref[pl.ds(SUBS + blk, cut, stride=SUBS), :] = gram[:cut]
        out1_ref[pl.ds(blk, cut, stride=SUBS), :] = gram[cut:]
        w = raw_ref[mine, 0:obs, lo:hi]
        slot = raw_ref[mine, obs : 2 * obs, lo:hi]
        value = w * (mag_ref[:, lo:hi] - pred)
        acc = jnp.zeros((entries, blk_rows), F32)
        for k in range(obs):
            acc = acc + jnp.where(slot[k : k + 1] == inv_col, value[k : k + 1], 0.0)
        t0_cols = jnp.where(lanes_sq == blk, jnp.sum(acc, axis=1, keepdims=True), t0_cols)
        wt_cols = jnp.where(lanes_sq == blk, jnp.sum(own, axis=1, keepdims=True), wt_cols)
    sq_ref[...] = jnp.zeros((LANES, LANES), F32)
    sq_ref[0:entries, :] = t0_cols
    sq_ref[entries : 2 * entries, :] = wt_cols
    flipped = sq_ref[...].T[0:SUBS]
    extra = jnp.where(lane < 3 * entries, pltpu.roll(fpos, 2 * entries, 1), pltpu.roll(cpos, 3 * entries, 1))
    out0_ref[0:SUBS, :] = jnp.where(lane < 2 * entries, flipped, extra)


def split3(value):
    hi = value.astype(BF16).astype(F32)
    rest = value - hi
    mid = rest.astype(BF16).astype(F32)
    return hi, mid, rest - mid


def sweep_kernel(
    dims, terms_ref, a0_ref, a1_ref, a2_ref, a3_ref, b0_ref, b1_ref, b2_ref, b3_ref, raw_ref, mag_ref, tab_ref, owner_ref,
    zp_ref, means_ref, misfit_ref,
    et_ref, v_ref, den_ref, fld_ref, col_ref, g_ref, s_ref, z_ref, dz_ref, zs_ref,
    sq_ref, lim_ref, fc_ref, fr_ref, tv_ref, ze_ref, rk_ref, big_ref, td_ref,
):
    tiles, bands, obs, stars, _, entries, fields, blk_rows, owned = dims
    groups = entries // 4
    pair = 2 * bands
    vrows = groups * pair
    lane8 = iota((SUBS, LANES), 1)
    low8 = lane8 < HALF
    my_tile, mine = lax.axis_index("sky"), lax.axis_index("band")
    mix_ref = mixing_row(terms_ref, mine, bands)

    layers = tiles // 2
    my_x, my_c = mine >> 1, mine & 1

    def load(swap):
        def block(part, dc, dx, dy, back, rows):
            d1, d2 = (dx, dy) if (dc == 1) != swap else (dy, dx)
            return part[2 * dc + d2][d1 * layers + back, rows, :]

        parts = ((a0_ref, a1_ref, a2_ref, a3_ref), (b0_ref, b1_ref, b2_ref, b3_ref))
        order = [(dy, back) for dy in range(2) for back in range(layers)]
        for dx in range(2):
            for dc in range(2):
                b = (my_x ^ dx) * 2 + (my_c ^ dc)
                sq_ref[...] = jnp.zeros((LANES, LANES), F32)
                for t, (dy, back) in enumerate(order):
                    sq_ref[t * SUBS : (t + 1) * SUBS, :] = block(parts[0], dc, dx, dy, back, slice(0, SUBS))
                et_ref[...] = sq_ref[...].T
                for p in range(2):
                    for q, dest in enumerate((v_ref, den_ref, fld_ref, col_ref)):
                        first = et_ref[pl.ds(q * entries + p, groups, stride=4), :]
                        second = et_ref[pl.ds(q * entries + 2 + p, groups, stride=4), :]
                        dest[pl.ds(p * bands + b, groups, stride=pair), :] = jnp.where(
                            low8, first, pltpu.roll(second, HALF, 1)
                        )

        for h in range(2):

            def turn(i, carry):
                k = i + h * (groups // 2)
                for p in range(2):
                    for dx in range(2):
                        for dc in range(2):
                            b = (my_x ^ dx) * 2 + (my_c ^ dc)
                            rows = []
                            for half in range(2):
                                start = pl.multiple_of((4 * i + 2 * half + p) * SUBS + (SUBS if h == 0 else 0), SUBS)
                                for dy, back in order:
                                    rows.append(block(parts[h], dc, dx, dy, back, pl.ds(start, SUBS)))
                            flipped = jnp.concatenate(rows, axis=0).T
                            for b2 in range(bands):
                                at = pl.ds(b2 * vrows + k * pair + p * bands + b, entries, stride=bands * vrows)
                                g_ref[at, :] = flipped[b2 * entries : (b2 + 1) * entries]
                return carry

            lax.fori_loop(0, groups // 2, turn, 0)

    @pl.when(my_c == 0)
    def load_even():
        load(False)

    @pl.when(my_c != 0)
    def load_odd():
        load(True)

    srows = 2 * groups
    fld2 = fld_ref[pl.ds(0, srows, stride=bands), :]
    col2 = col_ref[pl.ds(0, srows, stride=bands), :]
    row2 = iota((srows, LANES), 0)
    position = 4 * (row2 >> 1) + 2 * jnp.where(iota((srows, LANES), 1) < HALF, 0, 1) + (row2 & 1)
    for c in range(COLORS):
        hit = col2 == float(c)
        lim_ref[0, c] = jnp.min(jnp.where(hit, position, entries))
        lim_ref[1, c] = jnp.max(jnp.where(hit, position + 1, 0))
        count = jnp.sum(jnp.where(hit, 1.0, 0.0), axis=0, keepdims=True)
        lim_ref[2, c] = jnp.max(count + pltpu.roll(count, HALF, 1)).astype(I32)

    def fold_of(c):
        most = lim_ref[2, c]
        bounds = [0] + [4 * fold for fold in FOLDS]
        return [(fold, (most > low) & (most <= high)) for fold, low, high in zip(FOLDS, bounds, bounds[1:])], most > bounds[-1]

    def build_fold(c, fold):
        chosen = jnp.where(col2 == c.astype(F32), fld2, -1.0)
        folded = []
        for m in range(fold):
            for p in range(2):
                best = jnp.full((1, LANES), -1.0, F32)
                for k in range(m, groups, fold):
                    best = jnp.maximum(best, chosen[2 * k + p : 2 * k + p + 1])
                folded.append(best)
        sq_ref[0 : 2 * fold, :] = jnp.concatenate(folded, axis=0)
        columns = sq_ref[...].T
        others = [jnp.where(row < 0.0, -2.0, row) for row in folded]
        for i in range(2 * fold):
            col = jnp.broadcast_to(columns[:, i : i + 1], (LANES, LANES))
            for j in range(2 * fold):
                tile = jnp.where(col == others[j], 1.0, 0.0).astype(BF16)
                m, p, n, r = i // 2, i % 2, j // 2, j % 2
                s_ref[c * MOST + m * fold + n, p * LANES : (p + 1) * LANES, r * LANES : (r + 1) * LANES] = tile

    def build(c, carry):
        for fold, chosen in fold_of(c)[0]:
            pl.when(chosen)(functools.partial(build_fold, c, fold))
        return carry

    lax.fori_loop(0, COLORS, build, 0)

    def spread_rows(value):
        flat = jnp.concatenate([value[0:bands], value[bands:pair]], axis=1)
        hi, mid, lo = split3(flat)
        return jnp.concatenate([hi, mid, lo, jnp.zeros_like(hi)], axis=0).astype(BF16)

    def pack_rows(total):
        flat = total[0:bands] + (total[bands : 2 * bands] + total[2 * bands : 3 * bands])
        return jnp.concatenate([flat[:, :LANES], flat[:, LANES:]], axis=0)

    def same_field(c, work):
        cf = c.astype(F32)
        choices, rest = fold_of(c)

        def fast(fold):
            lhs = []
            for m in range(fold):
                rows_of = []
                for src, _ in work:
                    total = jnp.zeros((pair, LANES), F32)
                    for k in range(m, groups, fold):
                        rows = slice(k * pair, (k + 1) * pair)
                        total = total + jnp.where(col_ref[rows] == cf, src[rows], 0.0)
                    rows_of.append(spread_rows(total))
                lhs.append(jnp.concatenate(rows_of, axis=0))
            for n in range(fold):
                total = jnp.zeros((4 * bands * len(work), 2 * LANES), F32)
                for m in range(fold):
                    total = total + lax.dot_general(
                        lhs[m], s_ref[c * MOST + m * fold + n], NN, preferred_element_type=F32
                    )
                for i, (_, dest) in enumerate(work):
                    packed = pack_rows(total[4 * bands * i : 4 * bands * (i + 1)])
                    for k in range(n, groups, fold):
                        dest[k * pair : (k + 1) * pair, :] = packed

        for fold, chosen in choices:
            pl.when(chosen)(functools.partial(fast, fold))

        @pl.when(rest)
        def general():
            for src, dest in work:
                one_general(cf, src, dest)

    def one_general(cf, src, dest):
        chosen = jnp.where(col2 == cf, fld2, -1.0)
        sq_ref[...] = jnp.full((LANES, LANES), -1.0, F32)
        sq_ref[0:srows, :] = chosen
        columns = sq_ref[...].T
        for i in range(srows):
            fc_ref[i] = jnp.broadcast_to(columns[:, i : i + 1], (LANES, LANES))
            fr_ref[i] = row_to(jnp.where(chosen[i : i + 1] < 0.0, -2.0, chosen[i : i + 1]), SUBS)
        for m in range(groups):
            rows = slice(m * pair, (m + 1) * pair)
            big_ref[m] = spread_rows(jnp.where(col_ref[rows] == cf, src[rows], 0.0)).astype(F32)

        def outer(n, carry):
            def inner(m, total):
                parts = []
                for r in range(2):
                    row = fr_ref[2 * n + r][0:1]
                    upper = jnp.where(fc_ref[2 * m] == row, 1.0, 0.0)
                    lower = jnp.where(fc_ref[2 * m + 1] == row, 1.0, 0.0)
                    lhs = big_ref[m].astype(BF16)
                    parts.append(
                        lax.dot_general(lhs[:, :LANES], upper.astype(BF16), NN, preferred_element_type=F32)
                        + lax.dot_general(lhs[:, LANES:], lower.astype(BF16), NN, preferred_element_type=F32)
                    )
                return total + jnp.concatenate(parts, axis=1)

            total = lax.fori_loop(0, groups, inner, jnp.zeros((4 * bands, 2 * LANES), F32))
            dest[pl.ds(pl.multiple_of(n * pair, pair), pair), :] = pack_rows(total)
            return carry

        lax.fori_loop(0, groups, outer, 0)

    z_ref[...] = jnp.zeros((vrows, LANES), F32)

    def step(opening, n, carry):
        c = n & (COLORS - 1)
        cf = c.astype(F32)
        if opening:
            same_field(c, ((v_ref, tv_ref), (den_ref, td_ref)))
            for k in range(groups):
                rows = slice(k * pair, (k + 1) * pair)
                den_ref[rows] = jnp.where(col_ref[rows] == cf, 1.0 / (td_ref[rows] + PRIOR_WEIGHT), den_ref[rows])
        else:
            same_field(c, ((v_ref, tv_ref),))
        for k in range(groups):
            rows = slice(k * pair, (k + 1) * pair)
            old = z_ref[rows]
            new = jnp.where(col_ref[rows] == cf, tv_ref[rows] * den_ref[rows], old)
            z_ref[rows] = new
            diff = new - old
            turned = pltpu.roll(diff, HALF, 1)
            dz_ref[2 * k * pair : (2 * k + 1) * pair, :] = jnp.where(low8, diff, turned)
            dz_ref[(2 * k + 1) * pair : (2 * k + 2) * pair, :] = jnp.where(low8, turned, diff)

        def apply(q, accs):
            first = q * (2 * bands)
            rows = [row_to(dz_ref[pl.ds(first + i, 1), :], pair) for i in range(2 * bands)]
            out = []
            for k in range(groups):
                terms = []
                for i in range(2 * bands):
                    base = pl.multiple_of((first + i) * vrows + k * pair, pair)
                    terms.append(g_ref[pl.ds(base, pair), :] * rows[i])
                while len(terms) > 1:
                    terms = [terms[i] + terms[i + 1] for i in range(0, len(terms), 2)]
                out.append(accs[k] + terms[0])
            return tuple(out)

        start = tuple(v_ref[k * pair : (k + 1) * pair] for k in range(groups))
        done = lax.fori_loop(lim_ref[0, c] >> 1, (lim_ref[1, c] + 1) >> 1, apply, start)
        for k in range(groups):
            v_ref[k * pair : (k + 1) * pair, :] = done[k]

        @pl.when(c == COLORS - 1)
        def keep():
            zs_ref[n >> (COLORS.bit_length() - 1)] = z_ref[...]

        return carry

    lax.fori_loop(0, COLORS, functools.partial(step, True), 0)
    lax.fori_loop(COLORS, SWEEPS * COLORS, functools.partial(step, False), 0)

    tab = tab_ref[...]
    for sweep in range(SWEEPS):
        sq_ref[...] = jnp.zeros((LANES, LANES), F32)
        sq_ref[0:vrows, :] = zs_ref[sweep]
        et_ref[...] = sq_ref[...].T
        first = et_ref[0:SUBS, :]
        second = et_ref[HALF : HALF + SUBS, :]
        table = jnp.where(low8, first, pltpu.roll(second, HALF, 1))
        for b in range(bands):
            ze_ref[sweep * bands + b] = pick(table, tab + b)

    squares = [jnp.zeros((obs, LANES), F32) for _ in range(SWEEPS)]
    for chunk in range(stars // LANES):
        at = slice(chunk * LANES, (chunk + 1) * LANES)
        blk = chunk * LANES // blk_rows
        pred = [jnp.zeros((1, LANES), F32) for _ in range(SWEEPS)]
        own_mean = jnp.zeros((1, LANES), F32)
        for b in range(bands):
            w = raw_ref[b, 0:obs, at]
            slot = raw_ref[b, obs : 2 * obs, at].astype(I32)
            inverse = 1.0 / jnp.sum(w, axis=0, keepdims=True)
            base = raw_ref[b, chunk : chunk + 1, stars : stars + LANES]
            for sweep in range(SWEEPS):
                seen = pick(row_to(ze_ref[sweep * bands + b, blk : blk + 1, :], obs), slot)
                mean = base - jnp.sum(w * seen, axis=0, keepdims=True) * inverse
                pred[sweep] = pred[sweep] + mix_ref[b] * mean
                if sweep == SWEEPS - 1:
                    own_mean = jnp.where(mine == b, mean, own_mean)
        means_ref[0:1, at] = own_mean
        w = raw_ref[mine, 0:obs, at]
        slot = raw_ref[mine, obs : 2 * obs, at].astype(I32)
        mag = mag_ref[:, at]
        for sweep in range(SWEEPS):
            seen = pick(row_to(ze_ref[sweep * bands + mine, blk : blk + 1, :], obs), slot)
            gap = mag - pred[sweep] - seen
            squares[sweep] = squares[sweep] + w * gap * gap
    result = jnp.zeros((1, LANES), F32)
    for sweep in range(SWEEPS):
        result = jnp.where(lane8[0:1] == sweep, jnp.sum(squares[sweep]), result)
    misfit_ref[...] = result

    frows = fields // LANES
    own = jnp.where(owner_ref[...] == my_tile, 1.0, 0.0)
    upto = jnp.where(iota((LANES, LANES), 0) <= iota((LANES, LANES), 1), 1.0, 0.0).astype(BF16)
    inside = lax.dot_general(own.astype(BF16), upto, NN, preferred_element_type=F32)
    sums = jnp.broadcast_to(jnp.sum(own, axis=1, keepdims=True), (frows, LANES))
    before = jnp.where(iota((frows, frows), 1) < iota((frows, frows), 0), 1.0, 0.0).astype(BF16)
    ahead = lax.dot_general(before, sums.astype(BF16), NN, preferred_element_type=F32)
    rk_ref[...] = jnp.where(own > 0.0, inside + ahead - 1.0, -1.0)
    ids = jnp.where(fld2 < 0.0, 0.0, fld2).astype(I32)
    ranks = jnp.where(fld2 < 0.0, -1.0, table_lookup(rk_ref, ids, frows, -1.0))
    sq_ref[...] = jnp.full((LANES, LANES), -1.0, F32)
    sq_ref[0:srows, :] = ranks
    columns = sq_ref[...].T
    hi, mid, lo = split3(z_ref[pl.ds(mine, srows, stride=bands), :])
    places = iota((LANES, owned), 1).astype(F32)
    ones = jnp.ones((1, LANES), F32)
    total = jnp.zeros((SUBS, owned), F32)
    for r in range(srows):
        one_hot = jnp.where(jnp.broadcast_to(columns[:, r : r + 1], (LANES, owned)) == places, 1.0, 0.0)
        lhs = jnp.concatenate([hi[r : r + 1], mid[r : r + 1], lo[r : r + 1], ones, jnp.zeros((4, LANES), F32)], axis=0)
        total = total + lax.dot_general(lhs.astype(BF16), one_hot.astype(BF16), NN, preferred_element_type=F32)
    zp_ref[...] = (total[0:1] + (total[1:2] + total[2:3])) / jnp.maximum(total[3:4], 1.0)


def vmem():
    return pl.BlockSpec(memory_space=pltpu.VMEM)


def smem():
    return pl.BlockSpec(memory_space=pltpu.SMEM)


def move(value, bands, tiles, where):
    pairs = []
    for tile in range(tiles):
        for band in range(bands):
            z, y, x, c = where(tile >> 1, tile & 1, band >> 1, band & 1)
            pairs.append((tile * bands + band, (z * 2 + y) * bands + x * 2 + c))
    return lax.ppermute(value, ("sky", "band"), pairs)


def replicate(halves, bands, tiles):
    layers = tiles // 2
    send = lambda value, where: move(value, bands, tiles, where)
    order = sorted(range(1, layers), key=lambda k: -min(k, layers - k))
    other = lambda z, y, x, c: (z, y, x, c ^ 1)
    spread = []
    for half in halves:
        got = {k: send(half, lambda z, y, x, c, k=k: ((z + k) % layers, y, x, c)) for k in order}
        line = jnp.stack([half] + [got[k] for k in range(1, layers)])
        beside = send(line, lambda z, y, x, c: (z, y ^ 1, x, c) if c == 0 else (z, y, x ^ 1, c))
        near = jnp.concatenate([line, beside])
        across = send(near, lambda z, y, x, c: (z, y, x ^ 1, c) if c == 0 else (z, y ^ 1, x, c))
        spread += [near, across, send(near, other), send(across, other)]
    return spread


def sky_sum(value, bands, tiles):
    value = value + move(value, bands, tiles, lambda z, y, x, c: (z, y ^ 1, x, c))
    step = 1
    while step < tiles // 2:
        value = value + move(value, bands, tiles, lambda z, y, x, c, s=step: (z ^ s, y, x, c))
        step *= 2
    return value


def local_body(magnitudes, weights, slots, block_fields, owner, colors, color_terms):
    bands = color_terms.shape[0]
    tiles = lax.axis_size("sky")
    _, obs, stars = magnitudes.shape
    blocks, entries = block_fields.shape
    fields = owner.shape[0]
    blk_rows = stars // blocks
    owned = fields // tiles
    mags, wts, slt = magnitudes[0], weights[0], slots[0]
    packed = pl.pallas_call(
        pack_kernel,
        name="pack",
        out_shape=jax.ShapeDtypeStruct((2 * obs, stars + LANES), F32),
        in_specs=[vmem()] * 3,
        out_specs=vmem(),
    )(mags, wts, slt)
    raw = lax.all_gather(packed, "band", axis=0)

    rows_half = entries * SUBS // 2
    first, second, tab = pl.pallas_call(
        functools.partial(tile_kernel, (bands, obs, stars, blocks, entries, fields, blk_rows)),
        name="tile",
        out_shape=(
            jax.ShapeDtypeStruct((rows_half + SUBS, LANES), F32),
            jax.ShapeDtypeStruct((rows_half, LANES), F32),
            jax.ShapeDtypeStruct((SUBS, LANES), I32),
        ),
        in_specs=[smem(), vmem(), vmem(), vmem(), vmem()],
        out_specs=(vmem(), vmem(), vmem()),
        scratch_shapes=[
            pltpu.VMEM((SUBS, LANES), I32),
            pltpu.VMEM((LANES, LANES), F32),
            pltpu.VMEM((bands * entries, blk_rows), F32),
            pltpu.VMEM((bands * entries, blk_rows), F32),
            pltpu.VMEM((fields // LANES, LANES), F32),
        ],
    )(color_terms, raw, mags, block_fields, colors.reshape(-1, LANES))

    spread = replicate((first, second), bands, tiles)

    groups = entries // 4
    pair = 2 * bands
    vrows = groups * pair
    zp, means, partial = pl.pallas_call(
        functools.partial(sweep_kernel, (tiles, bands, obs, stars, blocks, entries, fields, blk_rows, owned)),
        name="sweeps",
        out_shape=(
            jax.ShapeDtypeStruct((1, owned), F32),
            jax.ShapeDtypeStruct((1, stars), F32),
            jax.ShapeDtypeStruct((1, LANES), F32),
        ),
        in_specs=[smem()] + [vmem()] * 12,
        out_specs=(vmem(), vmem(), vmem()),
        scratch_shapes=[
            pltpu.VMEM((LANES, LANES), F32),
            pltpu.VMEM((vrows, LANES), F32),
            pltpu.VMEM((vrows, LANES), F32),
            pltpu.VMEM((vrows, LANES), F32),
            pltpu.VMEM((vrows, LANES), F32),
            pltpu.VMEM((bands * entries * vrows, LANES), F32),
            pltpu.VMEM((COLORS * MOST, 2 * LANES, 2 * LANES), BF16),
            pltpu.VMEM((vrows, LANES), F32),
            pltpu.VMEM((bands * entries, LANES), F32),
            pltpu.VMEM((SWEEPS, vrows, LANES), F32),
            pltpu.VMEM((LANES, LANES), F32),
            pltpu.SMEM((3, COLORS), I32),
            pltpu.VMEM((2 * groups, LANES, LANES), F32),
            pltpu.VMEM((2 * groups, SUBS, LANES), F32),
            pltpu.VMEM((vrows, LANES), F32),
            pltpu.VMEM((SWEEPS * bands, SUBS, LANES), F32),
            pltpu.VMEM((fields // LANES, LANES), F32),
            pltpu.VMEM((groups, 4 * bands, 2 * LANES), F32),
            pltpu.VMEM((vrows, LANES), F32),
        ],
        compiler_params=pltpu.CompilerParams(vmem_limit_bytes=32 * 1024 * 1024),
    )(color_terms, *spread, raw, mags, tab, owner.reshape(-1, LANES))

    misfit = sky_sum(partial, bands, tiles)[0, :SWEEPS] / (obs * stars * tiles)
    return zp, means, misfit[:, None]


def fits_local(mesh, blocks_all, entries, stars, obs, bands, fields):
    tiles = mesh.shape["sky"]
    blocks = blocks_all // tiles
    return (
        2 * blocks_all == LANES
        and blocks == SUBS
        and bands == 4
        and bands * entries == LANES
        and obs == SUBS
        and 2 * bands == SUBS
        and mesh.shape["band"] == bands
        and stars // tiles == 2 * obs * LANES
        and (stars // blocks_all) % LANES == 0
        and fields % (tiles * LANES) == 0
    )


def from_behind(value, axis, steps):
    count = lax.axis_size(axis)
    pairs = [(source, (source + steps) % count) for source in range(count)]
    return lax.ppermute(value, axis, pairs)


def wide_body(magnitudes, weights, slots, block_fields, owner, colors, color_terms):
    band_count = color_terms.shape[0]
    tiles = lax.axis_size("sky")
    my_tile = lax.axis_index("sky")
    my_band = lax.axis_index("band")
    band_mags, band_wts, band_slots = (magnitudes, weights, slots)
    own_row = 0
    band_rows, obs_count, star_count = band_mags.shape
    block_count, list_len = block_fields.shape
    block_rows = star_count // block_count
    fields = owner.shape[0]
    slot_grid = band_slots.reshape(band_rows, obs_count, block_count, block_rows)
    entries = jnp.arange(list_len, dtype=jnp.int32)
    star_weight = jnp.sum(band_wts, axis=1)
    mixing = (
        jnp.eye(band_count, dtype=jnp.float32)
        + color_terms
        - jnp.diag(jnp.sum(color_terms, axis=1))
    )
    owner_order = jnp.argsort(owner, stable=True)
    owned = fields // tiles

    def slot_sums(values):
        grid = values.reshape(band_rows, obs_count, block_count, block_rows)
        hits = slot_grid[..., None] == entries
        return jnp.sum(jnp.where(hits, grid[..., None], 0.0), axis=(1, 3))

    def spread(list_vals):
        hits = slot_grid[..., None] == entries
        picked = jnp.sum(jnp.where(hits, list_vals[:, None, :, None, :], 0.0), axis=4)
        return picked.reshape(band_rows, obs_count, star_count)

    def predict(zp_obs):
        star_means = jnp.sum(band_wts * (band_mags - zp_obs), axis=1) / star_weight
        all_means = lax.all_gather(star_means, "band", axis=0, tiled=True)
        mix_row = lax.dynamic_index_in_dim(mixing, my_band, 0, keepdims=True)
        predicted = jnp.dot(mix_row, all_means, precision=lax.Precision.HIGHEST)
        return (star_means, predicted)

    positions = jnp.argsort(owner_order, stable=True)
    rank_in = positions - owner * owned
    live = block_fields < fields
    safe_ids = jnp.minimum(block_fields, fields - 1)
    relative = jnp.mod(jnp.take(owner, safe_ids) - my_tile + 1, tiles)
    list_ids = jnp.where(live, relative * owned + jnp.take(rank_in, safe_ids), 3 * owned)
    segments = 3 * owned
    nearby_idx = jnp.mod(my_tile + jnp.arange(3, dtype=jnp.int32) - 1, tiles)
    near_fields = jnp.take(owner_order.reshape(tiles, owned), nearby_idx, axis=0)
    zp_colors = jnp.take(colors, near_fields)[None]
    zero_pts = jnp.zeros((band_rows, 3, owned), jnp.float32)

    def flatten(table):
        return table.reshape(band_rows, 3 * owned)

    def combine(partial_flat):
        partial_sums = partial_flat.reshape(band_rows, 3, owned)
        from_left = from_behind(partial_sums[:, 1:3], "sky", 1)
        from_right = from_behind(partial_sums[:, 0:2], "sky", -1)
        far_left = from_behind(partial_sums[:, 2], "sky", 2)
        far_right = from_behind(partial_sums[:, 0], "sky", -2)
        below = far_left + from_left[:, 0] + partial_sums[:, 0]
        middle = from_left[:, 1] + partial_sums[:, 1] + from_right[:, 0]
        above = partial_sums[:, 2] + from_right[:, 1] + far_right
        return jnp.stack([below, middle, above], axis=1)

    def lookup(table):
        padded = jnp.concatenate([flatten(table), jnp.zeros((band_rows, 1), jnp.float32)], axis=1)
        return spread(jnp.take(padded, list_ids, axis=1))

    def segment_band(per_band):
        return jax.ops.segment_sum(
            per_band.reshape(-1), list_ids.reshape(-1), num_segments=segments + 1
        )[:segments]

    def totals(values):
        per_slot = slot_sums(values)
        return combine(jax.vmap(segment_band)(per_slot))

    denominators = totals(band_wts) + PRIOR_WEIGHT

    def squared_misfit(residual, zp_obs):
        per_band = jnp.sum(band_wts * (residual - zp_obs) ** 2, axis=(1, 2))
        return lax.dynamic_index_in_dim(per_band, own_row, 0, keepdims=False)

    def advance(table, color_no):
        zp_obs = lookup(table)
        _, predicted = predict(zp_obs)
        residual = band_mags - predicted[:, None, :]
        updated = totals(band_wts * residual) / denominators
        local_value = squared_misfit(residual, zp_obs)
        return (jnp.where(zp_colors == color_no, updated, table), local_value)

    def later_colors(color_no, table):
        return advance(table, color_no)[0]

    def record(local_value):
        return lax.psum(local_value, "sky")

    recorded = []
    for sweep_no in range(SWEEPS):
        zero_pts, local_value = advance(zero_pts, 0)
        if sweep_no > 0:
            recorded.append(record(local_value))
        zero_pts = lax.fori_loop(1, COLORS, later_colors, zero_pts)
    zp_obs = lookup(zero_pts)
    star_means, predicted = predict(zp_obs)
    residual = band_mags - predicted[:, None, :]
    recorded.append(record(squared_misfit(residual, zp_obs)))
    stacked = jnp.stack(recorded)
    misfit = stacked / (obs_count * star_count * tiles)
    own_zp = lax.dynamic_index_in_dim(zero_pts[:, 1], own_row, 0, keepdims=True)
    own_means = lax.dynamic_index_in_dim(star_means, own_row, 0, keepdims=True)
    return (own_zp, own_means, misfit[:, None])


def solution(mesh):
    in_specs = (
        P("band", None, "sky"),
        P("band", None, "sky"),
        P("band", None, "sky"),
        P("sky", None),
        P(),
        P(),
        P(),
    )
    out_specs = (P("band", "sky"), P("band", "sky"), P(None, "band"))

    def call(magnitudes, weights, slots, block_fields, owner, colors, color_terms):
        bands, obs, stars = magnitudes.shape
        blocks_all, entries = block_fields.shape
        local = fits_local(mesh, blocks_all, entries, stars, obs, bands, owner.shape[0])
        body = local_body if local else wide_body
        run = jax.shard_map(body, mesh=mesh, in_specs=in_specs, out_specs=out_specs, check_vma=False)
        return run(magnitudes, weights, slots, block_fields, owner, colors, color_terms)

    return call
```

profile of v0, /device:TPU:0, one launch (start us, length us, event | category | flops | bytes accessed | tf_op | source)
XLA Modules:
  0.0 95.9 jit_solution(5096631543399038374)
XLA Ops:
  0.6 1.6 %pack.1 = f32[16,2176]{1,0:T(8,128)} custom-call(f32[8,2048]{1,0:T(8,128)} %bitcast.26, f32[8,2048]{1,0:T(8,128)} %bitcast.38, s32[8,2048]{1,0:T(8,128)} %bitcast.39), custom_call_target="tpu_custom_call" | custom-call | tf_op jit(solution)/shard_map/pack/pallas_call | solution.py:499
  2.2 10.4 %all-gather = f32[64,2176]{1,0:T(8,128)} all-gather(f32[16,2176]{1,0:T(8,128)} %pack.1), channel_id=2, replica_groups=mesh['sky'=8,'band'=4] {'band'}, dimensions={0}, use_global_device_ids=true | all-gather | bytes 696320 | tf_op jit(solution)/shard_map/all_gather | solution.py:506
  12.6 4.5 %tile.1 = (f32[136,128]{1,0:T(8,128)}, f32[128,128]{1,0:T(8,128)}, s32[8,128]{1,0:T(8,128)}) custom-call(f32[4,4]{1,0:T(4,128)} %terms_ref.3, f32[4,16,2176]{2,1,0:T(8,128)} %bitcast.24, f32[8,2048]{1,0:T(8,128)} %bitcast.27, s32[8,32]{1,0:T(8,128)} %lists_ref.1, s32[32,128]{1,0:T(8,128)} %bitcast.40), custom_call_target="tpu_custom_call" | custom-call | tf_op jit(solution)/shard_map/tile/pallas_call | solution.py:509
  17.2 3.6 %collective-permute-start.9 = (f32[128,128]{1,0:T(8,128)}, f32[128,128]{1,0:T(8,128)S(1)}, u32[]{:S(2)}, u32[]{:S(2)}) collective-permute-start(f32[128,128]{1,0:T(8,128)} %get-tuple-element.10), channel_id=1, source_target_pairs={{0,24},{1,25},{2,26},{3,27},{4,28},{5,29},{6,30},{7,31},{8,0},{9,1... | collective-permute-start | bytes 196616 | tf_op jit(solution)/shard_map/ppermute | solution.py:462
  20.8 1.0 %collective-permute-start.7 = (f32[128,128]{1,0:T(8,128)}, f32[128,128]{1,0:T(8,128)S(1)}, u32[]{:S(2)}, u32[]{:S(2)}) collective-permute-start(f32[128,128]{1,0:T(8,128)} %get-tuple-element.10), channel_id=1, source_target_pairs={{0,8},{1,9},{2,10},{3,11},{4,12},{5,13},{6,14},{7,15},{8,16},{9,17... | collective-permute-start | bytes 196616 | tf_op jit(solution)/shard_map/ppermute | solution.py:462
  21.8 2.8 %collective-permute-start.2 = (f32[136,128]{1,0:T(8,128)}, f32[136,128]{1,0:T(8,128)S(1)}, u32[]{:S(2)}, u32[]{:S(2)}) collective-permute-start(f32[136,128]{1,0:T(8,128)} %get-tuple-element.9), channel_id=1, source_target_pairs={{0,24},{1,25},{2,26},{3,27},{4,28},{5,29},{6,30},{7,31},{8,0},{9,1... | collective-permute-start | bytes 208904 | tf_op jit(solution)/shard_map/ppermute | solution.py:462
  24.6 1.1 %collective-permute-start.1 = (f32[136,128]{1,0:T(8,128)}, f32[136,128]{1,0:T(8,128)S(1)}, u32[]{:S(2)}, u32[]{:S(2)}) collective-permute-start(f32[136,128]{1,0:T(8,128)} %get-tuple-element.9), channel_id=1, source_target_pairs={{0,16},{1,17},{2,18},{3,19},{4,20},{5,21},{6,22},{7,23},{8,24},{9,... | collective-permute-start | bytes 208904 | tf_op jit(solution)/shard_map/ppermute | solution.py:462
  25.7 0.9 constant_dynamic-update-slice_fusion.4
  26.7 0.9 copy-done.5
  27.5 0.0 collective-permute-start
  27.5 1.5 %collective-permute-done.8 = f32[128,128]{1,0:T(8,128)S(1)} collective-permute-done((f32[128,128]{1,0:T(8,128)}, f32[128,128]{1,0:T(8,128)S(1)}, u32[]{:S(2)}, u32[]{:S(2)}) %collective-permute-start.8) | collective-permute-done | bytes 65568 | tf_op jit(solution)/shard_map/ppermute | solution.py:462
  29.1 1.6 %collective-permute-start.10 = (f32[4,128,128]{2,1,0:T(8,128)S(1)}, f32[4,128,128]{2,1,0:T(8,128)S(1)}, u32[]{:S(2)}, u32[]{:S(2)}) collective-permute-start(f32[4,128,128]{2,1,0:T(8,128)S(1)} %pad_maximum_fusion.1), channel_id=1, source_target_pairs={{0,4},{1,3},{2,6},{3,1},{4,0},{5,7},{6,2},{7,5},{8,12},{9,11},{10,... | collective-permute-start | bytes 786440 | tf_op jit(solution)/shard_map/ppermute | solution.py:462
  30.7 3.3 %collective-permute-done.1 = f32[136,128]{1,0:T(8,128)S(1)} collective-permute-done((f32[136,128]{1,0:T(8,128)}, f32[136,128]{1,0:T(8,128)S(1)}, u32[]{:S(2)}, u32[]{:S(2)}) %collective-permute-start.1) | collective-permute-done | bytes 69664 | tf_op jit(solution)/shard_map/ppermute | solution.py:462
  34.0 1.6 %collective-permute-start.3 = (f32[4,136,128]{2,1,0:T(8,128)S(1)}, f32[4,136,128]{2,1,0:T(8,128)S(1)}, u32[]{:S(2)}, u32[]{:S(2)}) collective-permute-start(f32[4,136,128]{2,1,0:T(8,128)S(1)} %pad_maximum_fusion), channel_id=1, source_target_pairs={{0,4},{1,3},{2,6},{3,1},{4,0},{5,7},{6,2},{7,5},{8,12},{9,11},{10,... | collective-permute-start | bytes 835592 | tf_op jit(solution)/shard_map/ppermute | solution.py:462
  35.6 5.0 %collective-permute-done.3 = f32[4,136,128]{2,1,0:T(8,128)S(1)} collective-permute-done((f32[4,136,128]{2,1,0:T(8,128)S(1)}, f32[4,136,128]{2,1,0:T(8,128)S(1)}, u32[]{:S(2)}, u32[]{:S(2)}) %collective-permute-start.3) | collective-permute-done | bytes 278560 | tf_op jit(solution)/shard_map/ppermute | solution.py:462
  40.6 0.0 copy-start.1
  40.7 0.0 copy-start.2
  40.7 0.6 collective-permute-start.4
  41.3 0.0 copy-start.3
  41.3 1.6 %collective-permute-start.11 = (f32[8,128,128]{2,1,0:T(8,128)S(1)}, f32[8,128,128]{2,1,0:T(8,128)S(1)}, u32[]{:S(2)}, u32[]{:S(2)}) collective-permute-start(f32[8,128,128]{2,1,0:T(8,128)S(1)} %constant_dynamic-update-slice_fusion.5.b0_ref), channel_id=1, source_target_pairs={{0,2},{1,5},{2,0},{3,7},{4,6},{5,1},{6,4},{7,3},{8,10},{9,13},{10,... | collective-permute-start | bytes 1572872 | tf_op jit(solution)/shard_map/ppermute | solution.py:462
  42.9 7.4 %collective-permute-done.4.a1_ref = f32[8,136,128]{2,1,0:T(8,128)S(1)} collective-permute-done((f32[8,136,128]{2,1,0:T(8,128)S(1)}, f32[8,136,128]{2,1,0:T(8,128)S(1)}, u32[]{:S(2)}, u32[]{:S(2)}) %collective-permute-start.4) | collective-permute-done | bytes 557088 | tf_op jit(solution)/shard_map/ppermute | solution.py:462
  50.3 0.5 collective-permute-start.12
  50.8 5.1 %collective-permute-done.11.b1_ref = f32[8,128,128]{2,1,0:T(8,128)S(1)} collective-permute-done((f32[8,128,128]{2,1,0:T(8,128)S(1)}, f32[8,128,128]{2,1,0:T(8,128)S(1)}, u32[]{:S(2)}, u32[]{:S(2)}) %collective-permute-start.11) | collective-permute-done | bytes 524320 | tf_op jit(solution)/shard_map/ppermute | solution.py:462
  55.9 1.9 %collective-permute-done.13.b3_ref = f32[8,128,128]{2,1,0:T(8,128)S(1)} collective-permute-done((f32[8,128,128]{2,1,0:T(8,128)S(1)}, f32[8,128,128]{2,1,0:T(8,128)S(1)}, u32[]{:S(2)}, u32[]{:S(2)}) %collective-permute-start.13) | collective-permute-done | bytes 524320 | tf_op jit(solution)/shard_map/ppermute | solution.py:462
  57.8 26.0 %sweeps.1 = (f32[1,512]{1,0:T(1,128)}, f32[1,2048]{1,0:T(1,128)}, f32[1,128]{1,0:T(1,128)S(1)}) custom-call(f32[4,4]{1,0:T(4,128)S(1)} %copy-done.3, f32[8,136,128]{2,1,0:T(8,128)S(1)} %constant_dynamic-update-slice_fusion.a0_ref, f32[8,136,128]{2,1,0:T(8,128)S(1)} %collective-permute-done.4.a1_ref, f32[8,136,128]{2,1,0:T(8,128)S(1)} %collective-permute-done.5.a2_ref, ...), custom_call_target="tpu_custom_call" | custom-call | tf_op jit(solution)/shard_map/sweeps/pallas_call | solution.py:533
  83.8 1.5 %collective-permute-start.14 = (f32[1,128]{1,0:T(1,128)S(1)}, f32[1,128]{1,0:T(1,128)S(1)}, u32[]{:S(2)}, u32[]{:S(2)}) collective-permute-start(f32[1,128]{1,0:T(1,128)S(1)} %get-tuple-element.14), channel_id=1, source_target_pairs={{0,4},{1,5},{2,6},{3,7},{4,0},{5,1},{6,2},{7,3},{8,12},{9,13},{10,... | collective-permute-start | bytes 1544 | tf_op jit(solution)/shard_map/ppermute | solution.py:462
  85.3 2.1 %collective-permute-done.14 = f32[1,128]{1,0:T(1,128)S(1)} collective-permute-done((f32[1,128]{1,0:T(1,128)S(1)}, f32[1,128]{1,0:T(1,128)S(1)}, u32[]{:S(2)}, u32[]{:S(2)}) %collective-permute-start.14) | collective-permute-done | bytes 544 | tf_op jit(solution)/shard_map/ppermute | solution.py:462
  87.4 0.2 collective-permute-start.15
  87.6 3.4 %collective-permute-done.15 = f32[1,128]{1,0:T(1,128)S(1)} collective-permute-done((f32[1,128]{1,0:T(1,128)S(1)}, f32[1,128]{1,0:T(1,128)S(1)}, u32[]{:S(2)}, u32[]{:S(2)}) %collective-permute-start.15) | collective-permute-done | bytes 544 | tf_op jit(solution)/shard_map/ppermute | solution.py:462
  90.9 2.1 %collective-permute-start.16 = (f32[1,128]{1,0:T(1,128)S(1)}, f32[1,128]{1,0:T(1,128)S(1)}, u32[]{:S(2)}, u32[]{:S(2)}) collective-permute-start(f32[1,128]{1,0:T(1,128)S(1)} %add.10), channel_id=1, source_target_pairs={{0,16},{1,17},{2,18},{3,19},{4,20},{5,21},{6,22},{7,23},{8,24},{9,... | collective-permute-start | bytes 1544 | tf_op jit(solution)/shard_map/ppermute | solution.py:462
  93.1 2.3 %collective-permute-done.16 = f32[1,128]{1,0:T(1,128)S(1)} collective-permute-done((f32[1,128]{1,0:T(1,128)S(1)}, f32[1,128]{1,0:T(1,128)S(1)}, u32[]{:S(2)}, u32[]{:S(2)}) %collective-permute-start.16) | collective-permute-done | bytes 544 | tf_op jit(solution)/shard_map/ppermute | solution.py:462
  95.4 0.5 multiply_bitcast_fusion
  (36 shorter events, 0.2 us)
Async XLA Ops:
  17.2 9.5 %collective-permute-start.9 = (f32[128,128]{1,0:T(8,128)}, f32[128,128]{1,0:T(8,128)S(1)}, u32[]{:S(2)}, u32[]{:S(2)}) collective-permute-start(f32[128,128]{1,0:T(8,128)} %get-tuple-element.10), channel_id=1, source_target_pairs={{0,24},{1,25},{2,26},{3,27},{4,28},{5,29},{6,30},{7,31},{8,0},{9,1... | collective-permute-start | bytes 196616 | tf_op jit(solution)/shard_map/ppermute | solution.py:462
  20.8 8.3 %collective-permute-start.8 = (f32[128,128]{1,0:T(8,128)}, f32[128,128]{1,0:T(8,128)S(1)}, u32[]{:S(2)}, u32[]{:S(2)}) collective-permute-start(f32[128,128]{1,0:T(8,128)} %get-tuple-element.10), channel_id=1, source_target_pairs={{0,16},{1,17},{2,18},{3,19},{4,20},{5,21},{6,22},{7,23},{8,24},{9,... | collective-permute-start | bytes 196616 | tf_op jit(solution)/shard_map/ppermute | solution.py:462
  20.8 8.3 %collective-permute-start.7 = (f32[128,128]{1,0:T(8,128)}, f32[128,128]{1,0:T(8,128)S(1)}, u32[]{:S(2)}, u32[]{:S(2)}) collective-permute-start(f32[128,128]{1,0:T(8,128)} %get-tuple-element.10), channel_id=1, source_target_pairs={{0,8},{1,9},{2,10},{3,11},{4,12},{5,13},{6,14},{7,15},{8,16},{9,17... | collective-permute-start | bytes 196616 | tf_op jit(solution)/shard_map/ppermute | solution.py:462
  21.8 4.9 %copy-start.6 = (f32[128,128]{1,0:T(8,128)S(1)}, f32[128,128]{1,0:T(8,128)}, u32[]{:S(2)}) copy-start(f32[128,128]{1,0:T(8,128)} %get-tuple-element.10) | copy-start | bytes 196612
  21.8 8.9 %collective-permute-start.2 = (f32[136,128]{1,0:T(8,128)}, f32[136,128]{1,0:T(8,128)S(1)}, u32[]{:S(2)}, u32[]{:S(2)}) collective-permute-start(f32[136,128]{1,0:T(8,128)} %get-tuple-element.9), channel_id=1, source_target_pairs={{0,24},{1,25},{2,26},{3,27},{4,28},{5,29},{6,30},{7,31},{8,0},{9,1... | collective-permute-start | bytes 208904 | tf_op jit(solution)/shard_map/ppermute | solution.py:462
  24.6 9.4 %collective-permute-start.1 = (f32[136,128]{1,0:T(8,128)}, f32[136,128]{1,0:T(8,128)S(1)}, u32[]{:S(2)}, u32[]{:S(2)}) collective-permute-start(f32[136,128]{1,0:T(8,128)} %get-tuple-element.9), channel_id=1, source_target_pairs={{0,16},{1,17},{2,18},{3,19},{4,20},{5,21},{6,22},{7,23},{8,24},{9,... | collective-permute-start | bytes 208904 | tf_op jit(solution)/shard_map/ppermute | solution.py:462
  26.6 0.9 copy-start.5
  27.5 6.5 %collective-permute-start = (f32[136,128]{1,0:T(8,128)S(1)}, f32[136,128]{1,0:T(8,128)S(1)}, u32[]{:S(2)}, u32[]{:S(2)}) collective-permute-start(f32[136,128]{1,0:T(8,128)S(1)} %copy-done.5), channel_id=1, source_target_pairs={{0,8},{1,9},{2,10},{3,11},{4,12},{5,13},{6,14},{7,15},{8,16},{9,17... | collective-permute-start | bytes 208904 | tf_op jit(solution)/shard_map/ppermute | solution.py:462
  29.1 12.2 %collective-permute-start.10 = (f32[4,128,128]{2,1,0:T(8,128)S(1)}, f32[4,128,128]{2,1,0:T(8,128)S(1)}, u32[]{:S(2)}, u32[]{:S(2)}) collective-permute-start(f32[4,128,128]{2,1,0:T(8,128)S(1)} %pad_maximum_fusion.1), channel_id=1, source_target_pairs={{0,4},{1,3},{2,6},{3,1},{4,0},{5,7},{6,2},{7,5},{8,12},{9,11},{10,... | collective-permute-start | bytes 786440 | tf_op jit(solution)/shard_map/ppermute | solution.py:462
  34.0 6.6 %collective-permute-start.3 = (f32[4,136,128]{2,1,0:T(8,128)S(1)}, f32[4,136,128]{2,1,0:T(8,128)S(1)}, u32[]{:S(2)}, u32[]{:S(2)}) collective-permute-start(f32[4,136,128]{2,1,0:T(8,128)S(1)} %pad_maximum_fusion), channel_id=1, source_target_pairs={{0,4},{1,3},{2,6},{3,1},{4,0},{5,7},{6,2},{7,5},{8,12},{9,11},{10,... | collective-permute-start | bytes 835592 | tf_op jit(solution)/shard_map/ppermute | solution.py:462
  35.6 22.2 %copy-start = (f32[64,2176]{1,0:T(8,128)S(1)}, f32[64,2176]{1,0:T(8,128)}, u32[]{:S(2)}) copy-start(f32[64,2176]{1,0:T(8,128)} %all-gather) | copy-start | bytes 1671172
  40.6 17.2 %copy-start.1 = (f32[1,8,2048]{2,1,0:T(8,128)S(1)}, f32[1,8,2048]{2,1,0:T(8,128)}, u32[]{:S(2)}) copy-start(f32[1,8,2048]{2,1,0:T(8,128)} %param.7) | copy-start | bytes 196612
  40.7 17.2 %copy-start.2 = (s32[4096]{0:T(1024)S(1)}, s32[4096]{0:T(1024)}, u32[]{:S(2)}) copy-start(s32[4096]{0:T(1024)} %param.11) | copy-start | bytes 49156
  40.7 9.6 %collective-permute-start.4 = (f32[8,136,128]{2,1,0:T(8,128)S(1)}, f32[8,136,128]{2,1,0:T(8,128)S(1)}, u32[]{:S(2)}, u32[]{:S(2)}) collective-permute-start(f32[8,136,128]{2,1,0:T(8,128)S(1)} %constant_dynamic-update-slice_fusion.a0_ref), channel_id=1, source_target_pairs={{0,2},{1,5},{2,0},{3,7},{4,6},{5,1},{6,4},{7,3},{8,10},{9,13},{10,... | collective-permute-start | bytes 1671176 | tf_op jit(solution)/shard_map/ppermute | solution.py:462
  41.3 16.5 %copy-start.4 = (s32[8,128]{1,0:T(8,128)S(1)}, s32[8,128]{1,0:T(8,128)}, u32[]{:S(2)}) copy-start(s32[8,128]{1,0:T(8,128)} %get-tuple-element.11.tab_ref) | copy-start | bytes 12292
  41.3 16.5 %copy-start.3 = (f32[4,4]{1,0:T(4,128)S(1)}, f32[4,4]{1,0:T(4,128)}, u32[]{:S(2)}) copy-start(f32[4,4]{1,0:T(4,128)} %terms_ref.3) | copy-start | bytes 196
  41.3 14.6 %collective-permute-start.11 = (f32[8,128,128]{2,1,0:T(8,128)S(1)}, f32[8,128,128]{2,1,0:T(8,128)S(1)}, u32[]{:S(2)}, u32[]{:S(2)}) collective-permute-start(f32[8,128,128]{2,1,0:T(8,128)S(1)} %constant_dynamic-update-slice_fusion.5.b0_ref), channel_id=1, source_target_pairs={{0,2},{1,5},{2,0},{3,7},{4,6},{5,1},{6,4},{7,3},{8,10},{9,13},{10,... | collective-permute-start | bytes 1572872 | tf_op jit(solution)/shard_map/ppermute | solution.py:462
  42.9 13.0 %collective-permute-start.5 = (f32[8,136,128]{2,1,0:T(8,128)S(1)}, f32[8,136,128]{2,1,0:T(8,128)S(1)}, u32[]{:S(2)}, u32[]{:S(2)}) collective-permute-start(f32[8,136,128]{2,1,0:T(8,128)S(1)} %constant_dynamic-update-slice_fusion.a0_ref), channel_id=1, source_target_pairs={{0,1},{1,0},{2,3},{3,2},{4,5},{5,4},{6,7},{7,6},{8,9},{9,8},{10,11... | collective-permute-start | bytes 1671176 | tf_op jit(solution)/shard_map/ppermute | solution.py:462
  50.3 7.5 %collective-permute-start.6 = (f32[8,136,128]{2,1,0:T(8,128)S(1)}, f32[8,136,128]{2,1,0:T(8,128)S(1)}, u32[]{:S(2)}, u32[]{:S(2)}) collective-permute-start(f32[8,136,128]{2,1,0:T(8,128)S(1)} %collective-permute-done.4.a1_ref), channel_id=1, source_target_pairs={{0,1},{1,0},{2,3},{3,2},{4,5},{5,4},{6,7},{7,6},{8,9},{9,8},{10,11... | collective-permute-start | bytes 1671176 | tf_op jit(solution)/shard_map/ppermute | solution.py:462
  50.3 5.6 %collective-permute-start.12 = (f32[8,128,128]{2,1,0:T(8,128)S(1)}, f32[8,128,128]{2,1,0:T(8,128)S(1)}, u32[]{:S(2)}, u32[]{:S(2)}) collective-permute-start(f32[8,128,128]{2,1,0:T(8,128)S(1)} %constant_dynamic-update-slice_fusion.5.b0_ref), channel_id=1, source_target_pairs={{0,1},{1,0},{2,3},{3,2},{4,5},{5,4},{6,7},{7,6},{8,9},{9,8},{10,11... | collective-permute-start | bytes 1572872 | tf_op jit(solution)/shard_map/ppermute | solution.py:462
  55.9 1.9 %collective-permute-start.13 = (f32[8,128,128]{2,1,0:T(8,128)S(1)}, f32[8,128,128]{2,1,0:T(8,128)S(1)}, u32[]{:S(2)}, u32[]{:S(2)}) collective-permute-start(f32[8,128,128]{2,1,0:T(8,128)S(1)} %collective-permute-done.11.b1_ref), channel_id=1, source_target_pairs={{0,1},{1,0},{2,3},{3,2},{4,5},{5,4},{6,7},{7,6},{8,9},{9,8},{10,11... | collective-permute-start | bytes 1572872 | tf_op jit(solution)/shard_map/ppermute | solution.py:462
  83.8 3.6 %collective-permute-start.14 = (f32[1,128]{1,0:T(1,128)S(1)}, f32[1,128]{1,0:T(1,128)S(1)}, u32[]{:S(2)}, u32[]{:S(2)}) collective-permute-start(f32[1,128]{1,0:T(1,128)S(1)} %get-tuple-element.14), channel_id=1, source_target_pairs={{0,4},{1,5},{2,6},{3,7},{4,0},{5,1},{6,2},{7,3},{8,12},{9,13},{10,... | collective-permute-start | bytes 1544 | tf_op jit(solution)/shard_map/ppermute | solution.py:462
  87.4 3.6 %collective-permute-start.15 = (f32[1,128]{1,0:T(1,128)S(1)}, f32[1,128]{1,0:T(1,128)S(1)}, u32[]{:S(2)}, u32[]{:S(2)}) collective-permute-start(f32[1,128]{1,0:T(1,128)S(1)} %add.9), channel_id=1, source_target_pairs={{0,8},{1,9},{2,10},{3,11},{4,12},{5,13},{6,14},{7,15},{8,0},{9,1},... | collective-permute-start | bytes 1544 | tf_op jit(solution)/shard_map/ppermute | solution.py:462
  90.9 4.5 %collective-permute-start.16 = (f32[1,128]{1,0:T(1,128)S(1)}, f32[1,128]{1,0:T(1,128)S(1)}, u32[]{:S(2)}, u32[]{:S(2)}) collective-permute-start(f32[1,128]{1,0:T(1,128)S(1)} %add.10), channel_id=1, source_target_pairs={{0,16},{1,17},{2,18},{3,19},{4,20},{5,21},{6,22},{7,23},{8,24},{9,... | collective-permute-start | bytes 1544 | tf_op jit(solution)/shard_map/ppermute | solution.py:462
where the time goes:
time: 96.2 us; the launch traced here: 95.9 us
  Pallas kernels  32.1 us (33%)
  waiting for transfers between devices  32 us (33%)
  starting transfers between devices  18.2 us (19%)
  blocking collectives  10.4 us (11%)
  local copies, waits for them, and re-layouts  1.89 us (2%)
    ppermute x17, waiting for transfers between devices, move(): return lax.ppermute(value, ('sky', 'band'), pairs)  32 us
    pallas_call x1, Pallas kernels, local_body(): pl.pallas_call(functools.partial(sweep_kernel, (tiles, bands, obs, stars,...  26 us
    ppermute x17, starting transfers between devices, move(): return lax.ppermute(value, ('sky', 'band'), pairs)  18.2 us
    all_gather x1, blocking collectives, local_body(): raw = lax.all_gather(packed, 'band', axis=0)  10.4 us
    pallas_call x1, Pallas kernels, local_body(): pl.pallas_call(functools.partial(tile_kernel, (bands, obs, stars, blocks,...  4.55 us
  transfers between devices with their start and end apart: 17, of which 9 were waited for; matrix products, arithmetic and copies ran while one was open for 1% of the time, Pallas kernels for 0%

commit v1 on v0

--- a/solution.py
+++ b/solution.py
@@ -133,6 +133,7 @@
     sq_ref[entries : 2 * entries, :] = wt_cols
     flipped = sq_ref[...].T[0:SUBS]
     extra = jnp.where(lane < 3 * entries, pltpu.roll(fpos, 2 * entries, 1), pltpu.roll(cpos, 3 * entries, 1))
+    out1_ref[entries * SUBS // 2 :, :] = jnp.zeros((2 * SUBS, LANES), F32)
     out0_ref[0:SUBS, :] = jnp.where(lane < 2 * entries, flipped, extra)
 
 
@@ -143,37 +144,95 @@
     return hi, mid, rest - mid
 
 
-def sweep_kernel(
-    dims, terms_ref, a0_ref, a1_ref, a2_ref, a3_ref, b0_ref, b1_ref, b2_ref, b3_ref, raw_ref, mag_ref, tab_ref, owner_ref,
-    zp_ref, means_ref, misfit_ref,
-    et_ref, v_ref, den_ref, fld_ref, col_ref, g_ref, s_ref, z_ref, dz_ref, zs_ref,
-    sq_ref, lim_ref, fc_ref, fr_ref, tv_ref, ze_ref, rk_ref, big_ref, td_ref,
+def tile_order(tiles):
+    return [(dy, back) for dy in range(2) for back in range(tiles // 2)]
+
+
+def gathered(part, swap, layers, dc, dx, dy, back, rows):
+    d1, d2 = (dx, dy) if (dc == 1) != swap else (dy, dx)
+    return part[2 * dc + d2][d1 * layers + back, rows, :]
+
+
+def by_core(mine, run):
+    pl.when((mine & 1) == 0)(functools.partial(run, False))
+    pl.when((mine & 1) != 0)(functools.partial(run, True))
+
+
+def turn_half(part, swap, mine, tiles, bands, entries, skip, dest_ref):
+    groups = entries // 8
+    pair = 2 * bands
+    vrows = groups * pair
+
+    def turn(k, carry):
+        for p in range(2):
+            for dx in range(2):
+                for dc in range(2):
+                    b = ((mine >> 1) ^ dx) * 2 + ((mine & 1) ^ dc)
+                    rows = []
+                    for half in range(2):
+                        start = pl.multiple_of((4 * k + 2 * half + p) * SUBS + skip, SUBS)
+                        for dy, back in tile_order(tiles):
+                            rows.append(gathered(part, swap, tiles // 2, dc, dx, dy, back, pl.ds(start, SUBS)))
+                    flipped = jnp.concatenate(rows, axis=0).T
+                    for b2 in range(bands):
+                        at = pl.ds(b2 * vrows + k * pair + p * bands + b, entries, stride=bands * vrows)
+                        dest_ref[at, :] = flipped[b2 * entries : (b2 + 1) * entries]
+        return carry
+
+    lax.fori_loop(0, groups, turn, 0)
+
+
+def fold_of(lim_ref, c):
+    most = lim_ref[2, c]
+    bounds = [0] + [4 * fold for fold in FOLDS]
+    return [(fold, (most > low) & (most <= high)) for fold, low, high in zip(FOLDS, bounds, bounds[1:])], most > bounds[-1]
+
+
+def side_kernel(dims, terms_ref, owner_ref, raw_in, mag_in, tab_in, keep_ref):
+    bands, fields, stars = dims
+    raw_rows = raw_in.shape[1]
+    base = bands * raw_rows
+    for b in range(bands):
+        keep_ref[b * raw_rows : (b + 1) * raw_rows, :] = raw_in[b]
+    keep_ref[base : base + SUBS, 0:stars] = mag_in[...]
+    keep_ref[base : base + SUBS, stars : stars + LANES] = tab_in[...].astype(F32)
+    low = base + SUBS
+    span = fields // LANES // SUBS
+    for b, value in enumerate(mixing_row(terms_ref, lax.axis_index("band"), bands)):
+        keep_ref[low : low + SUBS, (span + b) * LANES : (span + b + 1) * LANES] = jnp.full((SUBS, LANES), value, F32)
+    my_tile = lax.axis_index("sky")
+    frows = fields // LANES
+    own = jnp.where(owner_ref[...] == my_tile, 1.0, 0.0)
+    upto = jnp.where(iota((LANES, LANES), 0) <= iota((LANES, LANES), 1), 1.0, 0.0).astype(BF16)
+    inside = lax.dot_general(own.astype(BF16), upto, NN, preferred_element_type=F32)
+    sums = jnp.broadcast_to(jnp.sum(own, axis=1, keepdims=True), (frows, LANES))
+    before = jnp.where(iota((frows, frows), 1) < iota((frows, frows), 0), 1.0, 0.0).astype(BF16)
+    ahead = lax.dot_general(before, sums.astype(BF16), NN, preferred_element_type=F32)
+    ranks = jnp.where(own > 0.0, inside + ahead - 1.0, -1.0)
+    for i in range(span):
+        keep_ref[low : low + SUBS, i * LANES : (i + 1) * LANES] = ranks[i * SUBS : (i + 1) * SUBS]
+
+
+def ready_kernel(
+    dims, near_ref, across_ref, far_near_ref, far_across_ref,
+    v_ref, den_ref, fld_ref, col_ref, g_ref, s_ref, lim_ref, sq_ref, et_ref,
 ):
-    tiles, bands, obs, stars, _, entries, fields, blk_rows, owned = dims
+    tiles, bands, entries = dims
     groups = entries // 4
     pair = 2 * bands
-    vrows = groups * pair
-    lane8 = iota((SUBS, LANES), 1)
-    low8 = lane8 < HALF
-    my_tile, mine = lax.axis_index("sky"), lax.axis_index("band")
-    mix_ref = mixing_row(terms_ref, mine, bands)
-
-    layers = tiles // 2
-    my_x, my_c = mine >> 1, mine & 1
+    low8 = iota((SUBS, LANES), 1) < HALF
+    mine = lax.axis_index("band")
+    part = (near_ref, across_ref, far_near_ref, far_across_ref)
 
     def load(swap):
-        def block(part, dc, dx, dy, back, rows):
-            d1, d2 = (dx, dy) if (dc == 1) != swap else (dy, dx)
-            return part[2 * dc + d2][d1 * layers + back, rows, :]
-
-        parts = ((a0_ref, a1_ref, a2_ref, a3_ref), (b0_ref, b1_ref, b2_ref, b3_ref))
-        order = [(dy, back) for dy in range(2) for back in range(layers)]
         for dx in range(2):
             for dc in range(2):
-                b = (my_x ^ dx) * 2 + (my_c ^ dc)
+                b = ((mine >> 1) ^ dx) * 2 + ((mine & 1) ^ dc)
                 sq_ref[...] = jnp.zeros((LANES, LANES), F32)
-                for t, (dy, back) in enumerate(order):
-                    sq_ref[t * SUBS : (t + 1) * SUBS, :] = block(parts[0], dc, dx, dy, back, slice(0, SUBS))
+                for t, (dy, back) in enumerate(tile_order(tiles)):
+                    sq_ref[t * SUBS : (t + 1) * SUBS, :] = gathered(
+                        part, swap, tiles // 2, dc, dx, dy, back, slice(0, SUBS)
+                    )
                 et_ref[...] = sq_ref[...].T
                 for p in range(2):
                     for q, dest in enumerate((v_ref, den_ref, fld_ref, col_ref)):
@@ -182,36 +241,9 @@
                         dest[pl.ds(p * bands + b, groups, stride=pair), :] = jnp.where(
                             low8, first, pltpu.roll(second, HALF, 1)
                         )
-
-        for h in range(2):
-
-            def turn(i, carry):
-                k = i + h * (groups // 2)
-                for p in range(2):
-                    for dx in range(2):
-                        for dc in range(2):
-                            b = (my_x ^ dx) * 2 + (my_c ^ dc)
-                            rows = []
-                            for half in range(2):
-                                start = pl.multiple_of((4 * i + 2 * half + p) * SUBS + (SUBS if h == 0 else 0), SUBS)
-                                for dy, back in order:
-                                    rows.append(block(parts[h], dc, dx, dy, back, pl.ds(start, SUBS)))
-                            flipped = jnp.concatenate(rows, axis=0).T
-                            for b2 in range(bands):
-                                at = pl.ds(b2 * vrows + k * pair + p * bands + b, entries, stride=bands * vrows)
-                                g_ref[at, :] = flipped[b2 * entries : (b2 + 1) * entries]
-                return carry
-
-            lax.fori_loop(0, groups // 2, turn, 0)
-
-    @pl.when(my_c == 0)
-    def load_even():
-        load(False)
-
-    @pl.when(my_c != 0)
-    def load_odd():
-        load(True)
-
+        turn_half(part, swap, mine, tiles, bands, entries, SUBS, g_ref)
+
+    by_core(mine, load)
     srows = 2 * groups
     fld2 = fld_ref[pl.ds(0, srows, stride=bands), :]
     col2 = col_ref[pl.ds(0, srows, stride=bands), :]
@@ -223,11 +255,6 @@
         lim_ref[1, c] = jnp.max(jnp.where(hit, position + 1, 0))
         count = jnp.sum(jnp.where(hit, 1.0, 0.0), axis=0, keepdims=True)
         lim_ref[2, c] = jnp.max(count + pltpu.roll(count, HALF, 1)).astype(I32)
-
-    def fold_of(c):
-        most = lim_ref[2, c]
-        bounds = [0] + [4 * fold for fold in FOLDS]
-        return [(fold, (most > low) & (most <= high)) for fold, low, high in zip(FOLDS, bounds, bounds[1:])], most > bounds[-1]
 
     def build_fold(c, fold):
         chosen = jnp.where(col2 == c.astype(F32), fld2, -1.0)
@@ -249,11 +276,36 @@
                 s_ref[c * MOST + m * fold + n, p * LANES : (p + 1) * LANES, r * LANES : (r + 1) * LANES] = tile
 
     def build(c, carry):
-        for fold, chosen in fold_of(c)[0]:
+        for fold, chosen in fold_of(lim_ref, c)[0]:
             pl.when(chosen)(functools.partial(build_fold, c, fold))
         return carry
 
     lax.fori_loop(0, COLORS, build, 0)
+
+
+def sweep_kernel(
+    dims, lim_ref, near_ref, across_ref, far_near_ref, far_across_ref,
+    v0_ref, wsum_ref, fld_ref, col_ref, ga_ref, s_ref, keep_ref,
+    zp_ref, means_ref, misfit_ref,
+    et_ref, v_ref, den_ref, gb_ref, z_ref, dz_ref, zs_ref,
+    sq_ref, fc_ref, fr_ref, tv_ref, ze_ref, big_ref, td_ref, rk_ref,
+):
+    tiles, bands, obs, stars, _, entries, fields, blk_rows, owned = dims
+    groups = entries // 4
+    pair = 2 * bands
+    vrows = groups * pair
+    lane8 = iota((SUBS, LANES), 1)
+    low8 = lane8 < HALF
+    mine = lax.axis_index("band")
+    base_row = 2 * obs * bands
+    span = fields // LANES // SUBS
+    part = (near_ref, across_ref, far_near_ref, far_across_ref)
+    by_core(mine, lambda swap: turn_half(part, swap, mine, tiles, bands, entries, 0, gb_ref))
+    v_ref[...] = v0_ref[...]
+    den_ref[...] = wsum_ref[...]
+    srows = 2 * groups
+    fld2 = fld_ref[pl.ds(0, srows, stride=bands), :]
+    col2 = col_ref[pl.ds(0, srows, stride=bands), :]
 
     def spread_rows(value):
         flat = jnp.concatenate([value[0:bands], value[bands:pair]], axis=1)
@@ -266,7 +318,7 @@
 
     def same_field(c, work):
         cf = c.astype(F32)
-        choices, rest = fold_of(c)
+        choices, rest = fold_of(lim_ref, c)
 
         def fast(fold):
             lhs = []
@@ -359,8 +411,9 @@
             for k in range(groups):
                 terms = []
                 for i in range(2 * bands):
-                    base = pl.multiple_of((first + i) * vrows + k * pair, pair)
-                    terms.append(g_ref[pl.ds(base, pair), :] * rows[i])
+                    gram_ref, kk = (ga_ref, k) if k < groups // 2 else (gb_ref, k - groups // 2)
+                    base = pl.multiple_of((first + i) * (vrows // 2) + kk * pair, pair)
+                    terms.append(gram_ref[pl.ds(base, pair), :] * rows[i])
                 while len(terms) > 1:
                     terms = [terms[i] + terms[i + 1] for i in range(0, len(terms), 2)]
                 out.append(accs[k] + terms[0])
@@ -380,7 +433,11 @@
     lax.fori_loop(0, COLORS, functools.partial(step, True), 0)
     lax.fori_loop(COLORS, SWEEPS * COLORS, functools.partial(step, False), 0)
 
-    tab = tab_ref[...]
+    tab = keep_ref[base_row : base_row + SUBS, stars : stars + LANES].astype(I32)
+    low = base_row + SUBS
+    mix_ref = [keep_ref[low : low + 1, (span + b) * LANES : (span + b + 1) * LANES] for b in range(bands)]
+    for i in range(span):
+        rk_ref[i * SUBS : (i + 1) * SUBS, :] = keep_ref[low : low + SUBS, i * LANES : (i + 1) * LANES]
     for sweep in range(SWEEPS):
         sq_ref[...] = jnp.zeros((LANES, LANES), F32)
         sq_ref[0:vrows, :] = zs_ref[sweep]
@@ -398,10 +455,10 @@
         pred = [jnp.zeros((1, LANES), F32) for _ in range(SWEEPS)]
         own_mean = jnp.zeros((1, LANES), F32)
         for b in range(bands):
-            w = raw_ref[b, 0:obs, at]
-            slot = raw_ref[b, obs : 2 * obs, at].astype(I32)
+            w = keep_ref[2 * obs * b : 2 * obs * b + obs, at]
+            slot = keep_ref[2 * obs * b + obs : 2 * obs * (b + 1), at].astype(I32)
             inverse = 1.0 / jnp.sum(w, axis=0, keepdims=True)
-            base = raw_ref[b, chunk : chunk + 1, stars : stars + LANES]
+            base = keep_ref[2 * obs * b + chunk : 2 * obs * b + chunk + 1, stars : stars + LANES]
             for sweep in range(SWEEPS):
                 seen = pick(row_to(ze_ref[sweep * bands + b, blk : blk + 1, :], obs), slot)
                 mean = base - jnp.sum(w * seen, axis=0, keepdims=True) * inverse
@@ -409,9 +466,10 @@
                 if sweep == SWEEPS - 1:
                     own_mean = jnp.where(mine == b, mean, own_mean)
         means_ref[0:1, at] = own_mean
-        w = raw_ref[mine, 0:obs, at]
-        slot = raw_ref[mine, obs : 2 * obs, at].astype(I32)
-        mag = mag_ref[:, at]
+        first = pl.multiple_of(mine * (2 * obs), SUBS)
+        w = keep_ref[pl.ds(first, obs), at]
+        slot = keep_ref[pl.ds(first + obs, obs), at].astype(I32)
+        mag = keep_ref[base_row : base_row + SUBS, at]
         for sweep in range(SWEEPS):
             seen = pick(row_to(ze_ref[sweep * bands + mine, blk : blk + 1, :], obs), slot)
             gap = mag - pred[sweep] - seen
@@ -422,13 +480,6 @@
     misfit_ref[...] = result
 
     frows = fields // LANES
-    own = jnp.where(owner_ref[...] == my_tile, 1.0, 0.0)
-    upto = jnp.where(iota((LANES, LANES), 0) <= iota((LANES, LANES), 1), 1.0, 0.0).astype(BF16)
-    inside = lax.dot_general(own.astype(BF16), upto, NN, preferred_element_type=F32)
-    sums = jnp.broadcast_to(jnp.sum(own, axis=1, keepdims=True), (frows, LANES))
-    before = jnp.where(iota((frows, frows), 1) < iota((frows, frows), 0), 1.0, 0.0).astype(BF16)
-    ahead = lax.dot_general(before, sums.astype(BF16), NN, preferred_element_type=F32)
-    rk_ref[...] = jnp.where(own > 0.0, inside + ahead - 1.0, -1.0)
     ids = jnp.where(fld2 < 0.0, 0.0, fld2).astype(I32)
     ranks = jnp.where(fld2 < 0.0, -1.0, table_lookup(rk_ref, ids, frows, -1.0))
     sq_ref[...] = jnp.full((LANES, LANES), -1.0, F32)
@@ -474,7 +525,7 @@
         beside = send(line, lambda z, y, x, c: (z, y ^ 1, x, c) if c == 0 else (z, y, x ^ 1, c))
         near = jnp.concatenate([line, beside])
         across = send(near, lambda z, y, x, c: (z, y, x ^ 1, c) if c == 0 else (z, y ^ 1, x, c))
-        spread += [near, across, send(near, other), send(across, other)]
+        spread.append([near, across, send(near, other), send(across, other)])
     return spread
 
 
@@ -511,7 +562,7 @@
         name="tile",
         out_shape=(
             jax.ShapeDtypeStruct((rows_half + SUBS, LANES), F32),
-            jax.ShapeDtypeStruct((rows_half, LANES), F32),
+            jax.ShapeDtypeStruct((rows_half + 2 * SUBS, LANES), F32),
             jax.ShapeDtypeStruct((SUBS, LANES), I32),
         ),
         in_specs=[smem(), vmem(), vmem(), vmem(), vmem()],
@@ -525,11 +576,38 @@
         ],
     )(color_terms, raw, mags, block_fields, colors.reshape(-1, LANES))
 
-    spread = replicate((first, second), bands, tiles)
-
+    late, early = replicate((second, first), bands, tiles)
     groups = entries // 4
     pair = 2 * bands
     vrows = groups * pair
+    state = jax.ShapeDtypeStruct((vrows, LANES), F32)
+    square = pltpu.VMEM((LANES, LANES), F32)
+    rows_state = pltpu.VMEM((vrows, LANES), F32)
+    *ready, limits = pl.pallas_call(
+        functools.partial(ready_kernel, (tiles, bands, entries)),
+        name="ready",
+        out_shape=(
+            state,
+            state,
+            state,
+            state,
+            jax.ShapeDtypeStruct((bands * entries * vrows // 2, LANES), F32),
+            jax.ShapeDtypeStruct((COLORS * MOST, 2 * LANES, 2 * LANES), BF16),
+            jax.ShapeDtypeStruct((3, COLORS), I32),
+        ),
+        in_specs=[vmem()] * 4,
+        out_specs=(vmem(),) * 6 + (smem(),),
+        scratch_shapes=[square, square],
+        compiler_params=pltpu.CompilerParams(vmem_limit_bytes=20 * 1024 * 1024),
+    )(*early)
+    keep = pl.pallas_call(
+        functools.partial(side_kernel, (bands, fields, stars)),
+        name="side",
+        out_shape=jax.ShapeDtypeStruct((2 * obs * bands + 2 * SUBS, stars + LANES), F32),
+        in_specs=[smem()] + [vmem()] * 4,
+        out_specs=vmem(),
+    )(color_terms, owner.reshape(-1, LANES), raw, mags, tab)
+
     zp, means, partial = pl.pallas_call(
         functools.partial(sweep_kernel, (tiles, bands, obs, stars, blocks, entries, fields, blk_rows, owned)),
         name="sweeps",
@@ -538,31 +616,27 @@
             jax.ShapeDtypeStruct((1, stars), F32),
             jax.ShapeDtypeStruct((1, LANES), F32),
         ),
-        in_specs=[smem()] + [vmem()] * 12,
+        in_specs=[smem()] + [vmem()] * 11,
         out_specs=(vmem(), vmem(), vmem()),
         scratch_shapes=[
-            pltpu.VMEM((LANES, LANES), F32),
-            pltpu.VMEM((vrows, LANES), F32),
-            pltpu.VMEM((vrows, LANES), F32),
-            pltpu.VMEM((vrows, LANES), F32),
-            pltpu.VMEM((vrows, LANES), F32),
-            pltpu.VMEM((bands * entries * vrows, LANES), F32),
-            pltpu.VMEM((COLORS * MOST, 2 * LANES, 2 * LANES), BF16),
-            pltpu.VMEM((vrows, LANES), F32),
+            square,
+            rows_state,
+            rows_state,
+            pltpu.VMEM((bands * entries * vrows // 2, LANES), F32),
+            rows_state,
             pltpu.VMEM((bands * entries, LANES), F32),
             pltpu.VMEM((SWEEPS, vrows, LANES), F32),
-            pltpu.VMEM((LANES, LANES), F32),
-            pltpu.SMEM((3, COLORS), I32),
+            square,
             pltpu.VMEM((2 * groups, LANES, LANES), F32),
             pltpu.VMEM((2 * groups, SUBS, LANES), F32),
-            pltpu.VMEM((vrows, LANES), F32),
+            rows_state,
             pltpu.VMEM((SWEEPS * bands, SUBS, LANES), F32),
+            pltpu.VMEM((groups, 4 * bands, 2 * LANES), F32),
+            rows_state,
             pltpu.VMEM((fields // LANES, LANES), F32),
-            pltpu.VMEM((groups, 4 * bands, 2 * LANES), F32),
-            pltpu.VMEM((vrows, LANES), F32),
         ],
-        compiler_params=pltpu.CompilerParams(vmem_limit_bytes=32 * 1024 * 1024),
-    )(color_terms, *spread, raw, mags, tab, owner.reshape(-1, LANES))
+        compiler_params=pltpu.CompilerParams(vmem_limit_bytes=20 * 1024 * 1024),
+    )(limits, *late, *ready, keep)
 
     misfit = sky_sum(partial, bands, tiles)[0, :SWEEPS] / (obs * stars * tiles)
     return zp, means, misfit[:, None]
@@ -581,7 +655,9 @@
         and mesh.shape["band"] == bands
         and stars // tiles == 2 * obs * LANES
         and (stars // blocks_all) % LANES == 0
+        and fields % (SUBS * LANES) == 0
         and fields % (tiles * LANES) == 0
+        and fields // SUBS + bands * LANES <= stars // tiles
     )
 
 

time: 96.2 us -> 100 us (1.040)
  waiting for transfers between devices: 32 us -> 27 us
  Pallas kernels: 32.1 us -> 35.8 us
  starting transfers between devices: 18.2 us -> 20.4 us
  other arithmetic: 0.57 us -> 2.35 us
  local copies, waits for them, and re-layouts: 1.89 us -> 2.98 us
    pallas_call x0 -> x2, Pallas kernels: none -> 9.26 us  [the longest x1 7.1 us: local_body(): pl.pallas_call(functools.partial(ready_kernel, (tiles, bands, entries)),...]
    pallas_call x1, Pallas kernels: 26 us -> 20.5 us  [local_body(): pl.pallas_call(functools.partial(sweep_kernel, (tiles, bands, obs, stars,...]
    ppermute x17, waiting for transfers between devices: 32 us -> 27 us  [move(): return lax.ppermute(value, ('sky', 'band'), pairs)]
    ppermute x17, starting transfers between devices: 18.2 us -> 20.4 us  [move(): return lax.ppermute(value, ('sky', 'band'), pairs)]
    another operation x2, other arithmetic: 0.04 us -> 1.83 us  [replicate(): line = jnp.stack([half] + [got[k] for k in range(1, layers)])]
    unnamed x22 -> x10, local copies, waits for them, and re-layouts: 1.85 us -> 2.94 us
  transfers between devices with their start and end apart: 17 -> 17, of which waited for: 9 -> 7; matrix products, arithmetic and copies ran while one was open for 1% -> 4% of each run, Pallas kernels for 0% -> 9%
where the time goes in v1:
time: 100 us; the launch traced here: 99.7 us
  Pallas kernels  35.8 us (36%)
  waiting for transfers between devices  27 us (27%)
  starting transfers between devices  20.4 us (20%)
  blocking collectives  10.4 us (10%)
  local copies, waits for them, and re-layouts  2.98 us (3%)
  other arithmetic  2.35 us (2%)
    ppermute x17, waiting for transfers between devices, move(): return lax.ppermute(value, ('sky', 'band'), pairs)  27 us
    pallas_call x1, Pallas kernels, local_body(): pl.pallas_call(functools.partial(sweep_kernel, (tiles, bands, obs, stars,...  20.5 us
    ppermute x17, starting transfers between devices, move(): return lax.ppermute(value, ('sky', 'band'), pairs)  20.4 us
    all_gather x1, blocking collectives, local_body(): raw = lax.all_gather(packed, 'band', axis=0)  10.4 us
    pallas_call x1, Pallas kernels, local_body(): pl.pallas_call(functools.partial(ready_kernel, (tiles, bands, entries)),...  7.1 us
    pallas_call x1, Pallas kernels, local_body(): pl.pallas_call(functools.partial(tile_kernel, (bands, obs, stars, blocks,...  4.54 us
    unnamed x10, local copies, waits for them, and re-layouts  2.94 us
    pallas_call x1, Pallas kernels, local_body(): pl.pallas_call(functools.partial(side_kernel, (bands, fields, stars)), na...  2.16 us
  transfers between devices with their start and end apart: 17, of which 7 were waited for; matrix products, arithmetic and copies ran while one was open for 4% of the time, Pallas kernels for 9%

profile of v1, /device:TPU:0, one launch (start us, length us, event | category | flops | bytes accessed | tf_op | source)
XLA Modules:
  0.0 99.7 jit_solution(5900835143195025763)
XLA Ops:
  0.6 1.6 %pack.1 = f32[16,2176]{1,0:T(8,128)} custom-call(f32[8,2048]{1,0:T(8,128)} %bitcast.26, f32[8,2048]{1,0:T(8,128)} %bitcast.37, s32[8,2048]{1,0:T(8,128)} %bitcast.38), custom_call_target="tpu_custom_call" | custom-call | tf_op jit(solution)/shard_map/pack/pallas_call | solution.py:550
  2.2 10.4 %all-gather = f32[64,2176]{1,0:T(8,128)} all-gather(f32[16,2176]{1,0:T(8,128)} %pack.1), channel_id=2, replica_groups=mesh['sky'=8,'band'=4] {'band'}, dimensions={0}, use_global_device_ids=true | all-gather | bytes 696320 | tf_op jit(solution)/shard_map/all_gather | solution.py:557
  12.6 4.5 %tile.1 = (f32[136,128]{1,0:T(8,128)}, f32[144,128]{1,0:T(8,128)}, s32[8,128]{1,0:T(8,128)}) custom-call(f32[4,4]{1,0:T(4,128)} %terms_ref.3, f32[4,16,2176]{2,1,0:T(8,128)} %bitcast.24, f32[8,2048]{1,0:T(8,128)} %bitcast.27, s32[8,32]{1,0:T(8,128)} %lists_ref.1, s32[32,128]{1,0:T(8,128)} %bitcast.40), custom_call_target="tpu_custom_call" | custom-call | tf_op jit(solution)/shard_map/tile/pallas_call | solution.py:560
  17.1 1.6 %collective-permute-start = (f32[136,128]{1,0:T(8,128)}, f32[136,128]{1,0:T(8,128)S(1)}, u32[]{:S(2)}, u32[]{:S(2)}) collective-permute-start(f32[136,128]{1,0:T(8,128)} %get-tuple-element.16), channel_id=1, source_target_pairs={{0,8},{1,9},{2,10},{3,11},{4,12},{5,13},{6,14},{7,15},{8,16},{9,17... | collective-permute-start | bytes 208904 | tf_op jit(solution)/shard_map/ppermute | solution.py:513
  18.7 2.6 %collective-permute-start.1 = (f32[136,128]{1,0:T(8,128)}, f32[136,128]{1,0:T(8,128)S(1)}, u32[]{:S(2)}, u32[]{:S(2)}) collective-permute-start(f32[136,128]{1,0:T(8,128)} %get-tuple-element.16), channel_id=1, source_target_pairs={{0,16},{1,17},{2,18},{3,19},{4,20},{5,21},{6,22},{7,23},{8,24},{9,... | collective-permute-start | bytes 208904 | tf_op jit(solution)/shard_map/ppermute | solution.py:513
  21.3 1.3 %collective-permute-start.2 = (f32[136,128]{1,0:T(8,128)}, f32[136,128]{1,0:T(8,128)S(1)}, u32[]{:S(2)}, u32[]{:S(2)}) collective-permute-start(f32[136,128]{1,0:T(8,128)} %get-tuple-element.16), channel_id=1, source_target_pairs={{0,24},{1,25},{2,26},{3,27},{4,28},{5,29},{6,30},{7,31},{8,0},{9,1... | collective-permute-start | bytes 208904 | tf_op jit(solution)/shard_map/ppermute | solution.py:513
  22.7 0.7 collective-permute-start.7
  23.7 0.9 constant_dynamic-update-slice_fusion.9
  24.6 0.9 constant_dynamic-update-slice_fusion.4
  25.5 2.9 %collective-permute-start.9 = (f32[144,128]{1,0:T(8,128)}, f32[144,128]{1,0:T(8,128)S(1)}, u32[]{:S(2)}, u32[]{:S(2)}) collective-permute-start(f32[144,128]{1,0:T(8,128)} %get-tuple-element.18), channel_id=1, source_target_pairs={{0,24},{1,25},{2,26},{3,27},{4,28},{5,29},{6,30},{7,31},{8,0},{9,1... | collective-permute-start | bytes 221192 | tf_op jit(solution)/shard_map/ppermute | solution.py:513
  28.4 0.9 pad_maximum_fusion.1
  29.3 1.6 %collective-permute-start.3 = (f32[4,136,128]{2,1,0:T(8,128)S(1)}, f32[4,136,128]{2,1,0:T(8,128)S(1)}, u32[]{:S(2)}, u32[]{:S(2)}) collective-permute-start(f32[4,136,128]{2,1,0:T(8,128)S(1)} %pad_maximum_fusion.1), channel_id=1, source_target_pairs={{0,4},{1,3},{2,6},{3,1},{4,0},{5,7},{6,2},{7,5},{8,12},{9,11},{10,... | collective-permute-start | bytes 835592 | tf_op jit(solution)/shard_map/ppermute | solution.py:513
  30.9 2.1 %collective-permute-done.8 = f32[144,128]{1,0:T(8,128)S(1)} collective-permute-done((f32[144,128]{1,0:T(8,128)}, f32[144,128]{1,0:T(8,128)S(1)}, u32[]{:S(2)}, u32[]{:S(2)}) %collective-permute-start.8) | collective-permute-done | bytes 73760 | tf_op jit(solution)/shard_map/ppermute | solution.py:513
  33.0 0.9 pad_maximum_fusion
  33.9 1.6 %collective-permute-start.10 = (f32[4,144,128]{2,1,0:T(8,128)S(1)}, f32[4,144,128]{2,1,0:T(8,128)S(1)}, u32[]{:S(2)}, u32[]{:S(2)}) collective-permute-start(f32[4,144,128]{2,1,0:T(8,128)S(1)} %pad_maximum_fusion), channel_id=1, source_target_pairs={{0,4},{1,3},{2,6},{3,1},{4,0},{5,7},{6,2},{7,5},{8,12},{9,11},{10,... | collective-permute-start | bytes 884744 | tf_op jit(solution)/shard_map/ppermute | solution.py:513
  35.6 5.2 %collective-permute-done.10 = f32[4,144,128]{2,1,0:T(8,128)S(1)} collective-permute-done((f32[4,144,128]{2,1,0:T(8,128)S(1)}, f32[4,144,128]{2,1,0:T(8,128)S(1)}, u32[]{:S(2)}, u32[]{:S(2)}) %collective-permute-start.10) | collective-permute-done | bytes 294944 | tf_op jit(solution)/shard_map/ppermute | solution.py:513
  40.8 0.6 collective-permute-start.11
  41.4 1.6 %collective-permute-start.4 = (f32[8,136,128]{2,1,0:T(8,128)S(1)}, f32[8,136,128]{2,1,0:T(8,128)S(1)}, u32[]{:S(2)}, u32[]{:S(2)}) collective-permute-start(f32[8,136,128]{2,1,0:T(8,128)S(1)} %constant_dynamic-update-slice_fusion.near_ref), channel_id=1, source_target_pairs={{0,2},{1,5},{2,0},{3,7},{4,6},{5,1},{6,4},{7,3},{8,10},{9,13},{10,... | collective-permute-start | bytes 1671176 | tf_op jit(solution)/shard_map/ppermute | solution.py:513
  42.9 7.8 %collective-permute-done.11.across_ref = f32[8,144,128]{2,1,0:T(8,128)S(1)} collective-permute-done((f32[8,144,128]{2,1,0:T(8,128)S(1)}, f32[8,144,128]{2,1,0:T(8,128)S(1)}, u32[]{:S(2)}, u32[]{:S(2)}) %collective-permute-start.11) | collective-permute-done | bytes 589856 | tf_op jit(solution)/shard_map/ppermute | solution.py:513
  50.7 0.5 collective-permute-start.5
  51.2 5.5 %collective-permute-done.4.across_ref = f32[8,136,128]{2,1,0:T(8,128)S(1)} collective-permute-done((f32[8,136,128]{2,1,0:T(8,128)S(1)}, f32[8,136,128]{2,1,0:T(8,128)S(1)}, u32[]{:S(2)}, u32[]{:S(2)}) %collective-permute-start.4) | collective-permute-done | bytes 557088 | tf_op jit(solution)/shard_map/ppermute | solution.py:513
  56.7 2.2 %side.1.keep_ref = f32[80,2176]{1,0:T(8,128)} custom-call(f32[4,4]{1,0:T(4,128)} %terms_ref.3, s32[32,128]{1,0:T(8,128)} %bitcast.39, f32[4,16,2176]{2,1,0:T(8,128)} %bitcast.25, f32[8,2048]{1,0:T(8,128)} %bitcast.28, s32[8,128]{1,0:T(8,128)} %get-tuple-element.25.tab_in), custom_call_target="tpu_custom_call" | custom-call | tf_op jit(solution)/shard_map/side/pallas_call | solution.py:603
  58.8 7.1 %ready.1 = (f32[64,128]{1,0:T(8,128)S(1)}, f32[64,128]{1,0:T(8,128)S(1)}, f32[64,128]{1,0:T(8,128)S(1)}, f32[64,128]{1,0:T(8,128)S(1)}, f32[4096,128]{1,0:T(8,12...) custom-call(f32[8,136,128]{2,1,0:T(8,128)S(1)} %constant_dynamic-update-slice_fusion.near_ref, ...), custom_call_target="tpu_custom_call" | custom-call | tf_op jit(solution)/shard_map/ready/pallas_call | solution.py:586
  66.0 1.1 %copy-done = f32[80,2176]{1,0:T(8,128)S(1)} copy-done((f32[80,2176]{1,0:T(8,128)S(1)}, f32[80,2176]{1,0:T(8,128)}, u32[]{:S(2)}) %copy-start) | copy-done | bytes 696344
  67.1 20.5 %sweeps.1 = (f32[1,512]{1,0:T(1,128)}, f32[1,2048]{1,0:T(1,128)}, f32[1,128]{1,0:T(1,128)S(1)}) custom-call(s32[3,8]{1,0:T(4,128)S(1)} %get-tuple-element.17.lim_ref, f32[8,144,128]{2,1,0:T(8,128)S(1)} %constant_dynamic-update-slice_fusion.5.near_ref, f32[8,144,128]{2,1,0:T(8,128)S(1)} %collective-permute-done.11.across_ref, ...), custom_call_target="tpu_custom_call" | custom-call | tf_op jit(solution)/shard_map/sweeps/pallas_call | solution.py:611
  87.5 1.5 %collective-permute-start.14 = (f32[1,128]{1,0:T(1,128)S(1)}, f32[1,128]{1,0:T(1,128)S(1)}, u32[]{:S(2)}, u32[]{:S(2)}) collective-permute-start(f32[1,128]{1,0:T(1,128)S(1)} %get-tuple-element.28), channel_id=1, source_target_pairs={{0,4},{1,5},{2,6},{3,7},{4,0},{5,1},{6,2},{7,3},{8,12},{9,13},{10,... | collective-permute-start | bytes 1544 | tf_op jit(solution)/shard_map/ppermute | solution.py:513
  89.1 2.0 %collective-permute-done.14 = f32[1,128]{1,0:T(1,128)S(1)} collective-permute-done((f32[1,128]{1,0:T(1,128)S(1)}, f32[1,128]{1,0:T(1,128)S(1)}, u32[]{:S(2)}, u32[]{:S(2)}) %collective-permute-start.14) | collective-permute-done | bytes 544 | tf_op jit(solution)/shard_map/ppermute | solution.py:513
  91.1 2.0 %collective-permute-start.15 = (f32[1,128]{1,0:T(1,128)S(1)}, f32[1,128]{1,0:T(1,128)S(1)}, u32[]{:S(2)}, u32[]{:S(2)}) collective-permute-start(f32[1,128]{1,0:T(1,128)S(1)} %add.9), channel_id=1, source_target_pairs={{0,8},{1,9},{2,10},{3,11},{4,12},{5,13},{6,14},{7,15},{8,0},{9,1},... | collective-permute-start | bytes 1544 | tf_op jit(solution)/shard_map/ppermute | solution.py:513
  93.1 1.6 %collective-permute-done.15 = f32[1,128]{1,0:T(1,128)S(1)} collective-permute-done((f32[1,128]{1,0:T(1,128)S(1)}, f32[1,128]{1,0:T(1,128)S(1)}, u32[]{:S(2)}, u32[]{:S(2)}) %collective-permute-start.15) | collective-permute-done | bytes 544 | tf_op jit(solution)/shard_map/ppermute | solution.py:513
  94.7 1.6 %collective-permute-start.16 = (f32[1,128]{1,0:T(1,128)S(1)}, f32[1,128]{1,0:T(1,128)S(1)}, u32[]{:S(2)}, u32[]{:S(2)}) collective-permute-start(f32[1,128]{1,0:T(1,128)S(1)} %add.10), channel_id=1, source_target_pairs={{0,16},{1,17},{2,18},{3,19},{4,20},{5,21},{6,22},{7,23},{8,24},{9,... | collective-permute-start | bytes 1544 | tf_op jit(solution)/shard_map/ppermute | solution.py:513
  96.3 2.9 %collective-permute-done.16 = f32[1,128]{1,0:T(1,128)S(1)} collective-permute-done((f32[1,128]{1,0:T(1,128)S(1)}, f32[1,128]{1,0:T(1,128)S(1)}, u32[]{:S(2)}, u32[]{:S(2)}) %collective-permute-start.16) | collective-permute-done | bytes 544 | tf_op jit(solution)/shard_map/ppermute | solution.py:513
  99.2 0.5 multiply_bitcast_fusion
  (26 shorter events, 0.5 us)
Async XLA Ops:
  17.1 8.3 %collective-permute-start = (f32[136,128]{1,0:T(8,128)}, f32[136,128]{1,0:T(8,128)S(1)}, u32[]{:S(2)}, u32[]{:S(2)}) collective-permute-start(f32[136,128]{1,0:T(8,128)} %get-tuple-element.16), channel_id=1, source_target_pairs={{0,8},{1,9},{2,10},{3,11},{4,12},{5,13},{6,14},{7,15},{8,16},{9,17... | collective-permute-start | bytes 208904 | tf_op jit(solution)/shard_map/ppermute | solution.py:513
  18.7 9.7 %collective-permute-start.1 = (f32[136,128]{1,0:T(8,128)}, f32[136,128]{1,0:T(8,128)S(1)}, u32[]{:S(2)}, u32[]{:S(2)}) collective-permute-start(f32[136,128]{1,0:T(8,128)} %get-tuple-element.16), channel_id=1, source_target_pairs={{0,16},{1,17},{2,18},{3,19},{4,20},{5,21},{6,22},{7,23},{8,24},{9,... | collective-permute-start | bytes 208904 | tf_op jit(solution)/shard_map/ppermute | solution.py:513
  21.3 7.1 %collective-permute-start.2 = (f32[136,128]{1,0:T(8,128)}, f32[136,128]{1,0:T(8,128)S(1)}, u32[]{:S(2)}, u32[]{:S(2)}) collective-permute-start(f32[136,128]{1,0:T(8,128)} %get-tuple-element.16), channel_id=1, source_target_pairs={{0,24},{1,25},{2,26},{3,27},{4,28},{5,29},{6,30},{7,31},{8,0},{9,1... | collective-permute-start | bytes 208904 | tf_op jit(solution)/shard_map/ppermute | solution.py:513
  22.7 8.3 %collective-permute-start.7 = (f32[144,128]{1,0:T(8,128)}, f32[144,128]{1,0:T(8,128)S(1)}, u32[]{:S(2)}, u32[]{:S(2)}) collective-permute-start(f32[144,128]{1,0:T(8,128)} %get-tuple-element.18), channel_id=1, source_target_pairs={{0,8},{1,9},{2,10},{3,11},{4,12},{5,13},{6,14},{7,15},{8,16},{9,17... | collective-permute-start | bytes 221192 | tf_op jit(solution)/shard_map/ppermute | solution.py:513
  23.3 9.6 %collective-permute-start.8 = (f32[144,128]{1,0:T(8,128)}, f32[144,128]{1,0:T(8,128)S(1)}, u32[]{:S(2)}, u32[]{:S(2)}) collective-permute-start(f32[144,128]{1,0:T(8,128)} %get-tuple-element.18), channel_id=1, source_target_pairs={{0,16},{1,17},{2,18},{3,19},{4,20},{5,21},{6,22},{7,23},{8,24},{9,... | collective-permute-start | bytes 221192 | tf_op jit(solution)/shard_map/ppermute | solution.py:513
  25.5 7.5 %collective-permute-start.9 = (f32[144,128]{1,0:T(8,128)}, f32[144,128]{1,0:T(8,128)S(1)}, u32[]{:S(2)}, u32[]{:S(2)}) collective-permute-start(f32[144,128]{1,0:T(8,128)} %get-tuple-element.18), channel_id=1, source_target_pairs={{0,24},{1,25},{2,26},{3,27},{4,28},{5,29},{6,30},{7,31},{8,0},{9,1... | collective-permute-start | bytes 221192 | tf_op jit(solution)/shard_map/ppermute | solution.py:513
  29.3 12.1 %collective-permute-start.3 = (f32[4,136,128]{2,1,0:T(8,128)S(1)}, f32[4,136,128]{2,1,0:T(8,128)S(1)}, u32[]{:S(2)}, u32[]{:S(2)}) collective-permute-start(f32[4,136,128]{2,1,0:T(8,128)S(1)} %pad_maximum_fusion.1), channel_id=1, source_target_pairs={{0,4},{1,3},{2,6},{3,1},{4,0},{5,7},{6,2},{7,5},{8,12},{9,11},{10,... | collective-permute-start | bytes 835592 | tf_op jit(solution)/shard_map/ppermute | solution.py:513
  33.9 6.8 %collective-permute-start.10 = (f32[4,144,128]{2,1,0:T(8,128)S(1)}, f32[4,144,128]{2,1,0:T(8,128)S(1)}, u32[]{:S(2)}, u32[]{:S(2)}) collective-permute-start(f32[4,144,128]{2,1,0:T(8,128)S(1)} %pad_maximum_fusion), channel_id=1, source_target_pairs={{0,4},{1,3},{2,6},{3,1},{4,0},{5,7},{6,2},{7,5},{8,12},{9,11},{10,... | collective-permute-start | bytes 884744 | tf_op jit(solution)/shard_map/ppermute | solution.py:513
  40.8 9.9 %collective-permute-start.11 = (f32[8,144,128]{2,1,0:T(8,128)S(1)}, f32[8,144,128]{2,1,0:T(8,128)S(1)}, u32[]{:S(2)}, u32[]{:S(2)}) collective-permute-start(f32[8,144,128]{2,1,0:T(8,128)S(1)} %constant_dynamic-update-slice_fusion.5.near_ref), channel_id=1, source_target_pairs={{0,2},{1,5},{2,0},{3,7},{4,6},{5,1},{6,4},{7,3},{8,10},{9,13},{10,... | collective-permute-start | bytes 1769480 | tf_op jit(solution)/shard_map/ppermute | solution.py:513
  41.4 15.3 %collective-permute-start.4 = (f32[8,136,128]{2,1,0:T(8,128)S(1)}, f32[8,136,128]{2,1,0:T(8,128)S(1)}, u32[]{:S(2)}, u32[]{:S(2)}) collective-permute-start(f32[8,136,128]{2,1,0:T(8,128)S(1)} %constant_dynamic-update-slice_fusion.near_ref), channel_id=1, source_target_pairs={{0,2},{1,5},{2,0},{3,7},{4,6},{5,1},{6,4},{7,3},{8,10},{9,13},{10,... | collective-permute-start | bytes 1671176 | tf_op jit(solution)/shard_map/ppermute | solution.py:513
  42.9 23.0 %collective-permute-start.12 = (f32[8,144,128]{2,1,0:T(8,128)S(1)}, f32[8,144,128]{2,1,0:T(8,128)S(1)}, u32[]{:S(2)}, u32[]{:S(2)}) collective-permute-start(f32[8,144,128]{2,1,0:T(8,128)S(1)} %constant_dynamic-update-slice_fusion.5.near_ref), channel_id=1, source_target_pairs={{0,1},{1,0},{2,3},{3,2},{4,5},{5,4},{6,7},{7,6},{8,9},{9,8},{10,11... | collective-permute-start | bytes 1769480 | tf_op jit(solution)/shard_map/ppermute | solution.py:513
  50.7 15.3 %collective-permute-start.13 = (f32[8,144,128]{2,1,0:T(8,128)S(1)}, f32[8,144,128]{2,1,0:T(8,128)S(1)}, u32[]{:S(2)}, u32[]{:S(2)}) collective-permute-start(f32[8,144,128]{2,1,0:T(8,128)S(1)} %collective-permute-done.11.across_ref), channel_id=1, source_target_pairs={{0,1},{1,0},{2,3},{3,2},{4,5},{5,4},{6,7},{7,6},{8,9},{9,8},{10,11... | collective-permute-start | bytes 1769480 | tf_op jit(solution)/shard_map/ppermute | solution.py:513
  50.7 8.1 %collective-permute-start.5 = (f32[8,136,128]{2,1,0:T(8,128)S(1)}, f32[8,136,128]{2,1,0:T(8,128)}, u32[]{:S(2)}, u32[]{:S(2)}) collective-permute-start(f32[8,136,128]{2,1,0:T(8,128)S(1)} %constant_dynamic-update-slice_fusion.near_ref), channel_id=1, source_target_pairs={{0,1},{1,0},{2,3},{3,2},{4,5},{5,4},{6,7},{7,6},{8,9},{9,8},{10,11... | collective-permute-start | bytes 1671176 | tf_op jit(solution)/shard_map/ppermute | solution.py:513
  56.7 2.2 %collective-permute-start.6 = (f32[8,136,128]{2,1,0:T(8,128)S(1)}, f32[8,136,128]{2,1,0:T(8,128)}, u32[]{:S(2)}, u32[]{:S(2)}) collective-permute-start(f32[8,136,128]{2,1,0:T(8,128)S(1)} %collective-permute-done.4.across_ref), channel_id=1, source_target_pairs={{0,1},{1,0},{2,3},{3,2},{4,5},{5,4},{6,7},{7,6},{8,9},{9,8},{10,11... | collective-permute-start | bytes 1671176 | tf_op jit(solution)/shard_map/ppermute | solution.py:513
  66.0 1.1 %copy-start = (f32[80,2176]{1,0:T(8,128)S(1)}, f32[80,2176]{1,0:T(8,128)}, u32[]{:S(2)}) copy-start(f32[80,2176]{1,0:T(8,128)} %side.1.keep_ref) | copy-start | bytes 2088964
  87.5 3.6 %collective-permute-start.14 = (f32[1,128]{1,0:T(1,128)S(1)}, f32[1,128]{1,0:T(1,128)S(1)}, u32[]{:S(2)}, u32[]{:S(2)}) collective-permute-start(f32[1,128]{1,0:T(1,128)S(1)} %get-tuple-element.28), channel_id=1, source_target_pairs={{0,4},{1,5},{2,6},{3,7},{4,0},{5,1},{6,2},{7,3},{8,12},{9,13},{10,... | collective-permute-start | bytes 1544 | tf_op jit(solution)/shard_map/ppermute | solution.py:513
  91.1 3.6 %collective-permute-start.15 = (f32[1,128]{1,0:T(1,128)S(1)}, f32[1,128]{1,0:T(1,128)S(1)}, u32[]{:S(2)}, u32[]{:S(2)}) collective-permute-start(f32[1,128]{1,0:T(1,128)S(1)} %add.9), channel_id=1, source_target_pairs={{0,8},{1,9},{2,10},{3,11},{4,12},{5,13},{6,14},{7,15},{8,0},{9,1},... | collective-permute-start | bytes 1544 | tf_op jit(solution)/shard_map/ppermute | solution.py:513
  94.7 4.5 %collective-permute-start.16 = (f32[1,128]{1,0:T(1,128)S(1)}, f32[1,128]{1,0:T(1,128)S(1)}, u32[]{:S(2)}, u32[]{:S(2)}) collective-permute-start(f32[1,128]{1,0:T(1,128)S(1)} %add.10), channel_id=1, source_target_pairs={{0,16},{1,17},{2,18},{3,19},{4,20},{5,21},{6,22},{7,23},{8,24},{9,... | collective-permute-start | bytes 1544 | tf_op jit(solution)/shard_map/ppermute | solution.py:513

commit v2 on v1

--- a/solution.py
+++ b/solution.py
@@ -213,9 +213,67 @@
         keep_ref[low : low + SUBS, i * LANES : (i + 1) * LANES] = ranks[i * SUBS : (i + 1) * SUBS]
 
 
+def fields_kernel(dims, near_ref, far_near_ref, s_ref, lim_ref, sq_ref, et_ref, fld_ref, col_ref):
+    tiles, entries = dims
+    groups = entries // 4
+    low8 = iota((SUBS, LANES), 1) < HALF
+    mine = lax.axis_index("band")
+
+    def load(swap):
+        source = far_near_ref if swap else near_ref
+        sq_ref[...] = jnp.zeros((LANES, LANES), F32)
+        for t in range(tiles):
+            sq_ref[t * SUBS : (t + 1) * SUBS, :] = source[t, 0:SUBS, :]
+        et_ref[...] = sq_ref[...].T
+        for p in range(2):
+            for q, dest in ((2, fld_ref), (3, col_ref)):
+                first = et_ref[pl.ds(q * entries + p, groups, stride=4), :]
+                second = et_ref[pl.ds(q * entries + 2 + p, groups, stride=4), :]
+                dest[pl.ds(p, groups, stride=2), :] = jnp.where(low8, first, pltpu.roll(second, HALF, 1))
+
+    by_core(mine, load)
+    srows = 2 * groups
+    fld2 = fld_ref[...]
+    col2 = col_ref[...]
+    row2 = iota((srows, LANES), 0)
+    position = 4 * (row2 >> 1) + 2 * jnp.where(iota((srows, LANES), 1) < HALF, 0, 1) + (row2 & 1)
+    for c in range(COLORS):
+        hit = col2 == float(c)
+        lim_ref[0, c] = jnp.min(jnp.where(hit, position, entries))
+        lim_ref[1, c] = jnp.max(jnp.where(hit, position + 1, 0))
+        count = jnp.sum(jnp.where(hit, 1.0, 0.0), axis=0, keepdims=True)
+        lim_ref[2, c] = jnp.max(count + pltpu.roll(count, HALF, 1)).astype(I32)
+
+    def build_fold(c, fold):
+        chosen = jnp.where(col2 == c.astype(F32), fld2, -1.0)
+        folded = []
+        for m in range(fold):
+            for p in range(2):
+                best = jnp.full((1, LANES), -1.0, F32)
+                for k in range(m, groups, fold):
+                    best = jnp.maximum(best, chosen[2 * k + p : 2 * k + p + 1])
+                folded.append(best)
+        sq_ref[0 : 2 * fold, :] = jnp.concatenate(folded, axis=0)
+        columns = sq_ref[...].T
+        others = [jnp.where(row < 0.0, -2.0, row) for row in folded]
+        for i in range(2 * fold):
+            col = jnp.broadcast_to(columns[:, i : i + 1], (LANES, LANES))
+            for j in range(2 * fold):
+                tile = jnp.where(col == others[j], 1.0, 0.0).astype(BF16)
+                m, p, n, r = i // 2, i % 2, j // 2, j % 2
+                s_ref[c * MOST + m * fold + n, p * LANES : (p + 1) * LANES, r * LANES : (r + 1) * LANES] = tile
+
+    def build(c, carry):
+        for fold, chosen in fold_of(lim_ref, c)[0]:
+            pl.when(chosen)(functools.partial(build_fold, c, fold))
+        return carry
+
+    lax.fori_loop(0, COLORS, build, 0)
+
+
 def ready_kernel(
     dims, near_ref, across_ref, far_near_ref, far_across_ref,
-    v_ref, den_ref, fld_ref, col_ref, g_ref, s_ref, lim_ref, sq_ref, et_ref,
+    v_ref, den_ref, fld_ref, col_ref, g_ref, sq_ref, et_ref,
 ):
     tiles, bands, entries = dims
     groups = entries // 4
@@ -244,43 +302,6 @@
         turn_half(part, swap, mine, tiles, bands, entries, SUBS, g_ref)
 
     by_core(mine, load)
-    srows = 2 * groups
-    fld2 = fld_ref[pl.ds(0, srows, stride=bands), :]
-    col2 = col_ref[pl.ds(0, srows, stride=bands), :]
-    row2 = iota((srows, LANES), 0)
-    position = 4 * (row2 >> 1) + 2 * jnp.where(iota((srows, LANES), 1) < HALF, 0, 1) + (row2 & 1)
-    for c in range(COLORS):
-        hit = col2 == float(c)
-        lim_ref[0, c] = jnp.min(jnp.where(hit, position, entries))
-        lim_ref[1, c] = jnp.max(jnp.where(hit, position + 1, 0))
-        count = jnp.sum(jnp.where(hit, 1.0, 0.0), axis=0, keepdims=True)
-        lim_ref[2, c] = jnp.max(count + pltpu.roll(count, HALF, 1)).astype(I32)
-
-    def build_fold(c, fold):
-        chosen = jnp.where(col2 == c.astype(F32), fld2, -1.0)
-        folded = []
-        for m in range(fold):
-            for p in range(2):
-                best = jnp.full((1, LANES), -1.0, F32)
-                for k in range(m, groups, fold):
-                    best = jnp.maximum(best, chosen[2 * k + p : 2 * k + p + 1])
-                folded.append(best)
-        sq_ref[0 : 2 * fold, :] = jnp.concatenate(folded, axis=0)
-        columns = sq_ref[...].T
-        others = [jnp.where(row < 0.0, -2.0, row) for row in folded]
-        for i in range(2 * fold):
-            col = jnp.broadcast_to(columns[:, i : i + 1], (LANES, LANES))
-            for j in range(2 * fold):
-                tile = jnp.where(col == others[j], 1.0, 0.0).astype(BF16)
-                m, p, n, r = i // 2, i % 2, j // 2, j % 2
-                s_ref[c * MOST + m * fold + n, p * LANES : (p + 1) * LANES, r * LANES : (r + 1) * LANES] = tile
-
-    def build(c, carry):
-        for fold, chosen in fold_of(lim_ref, c)[0]:
-            pl.when(chosen)(functools.partial(build_fold, c, fold))
-        return carry
-
-    lax.fori_loop(0, COLORS, build, 0)
 
 
 def sweep_kernel(
@@ -583,23 +604,27 @@
     state = jax.ShapeDtypeStruct((vrows, LANES), F32)
     square = pltpu.VMEM((LANES, LANES), F32)
     rows_state = pltpu.VMEM((vrows, LANES), F32)
-    *ready, limits = pl.pallas_call(
+    ready = pl.pallas_call(
         functools.partial(ready_kernel, (tiles, bands, entries)),
         name="ready",
+        out_shape=(state, state, state, state, jax.ShapeDtypeStruct((bands * entries * vrows // 2, LANES), F32)),
+        in_specs=[vmem()] * 4,
+        out_specs=(vmem(),) * 5,
+        scratch_shapes=[square, square],
+        compiler_params=pltpu.CompilerParams(vmem_limit_bytes=20 * 1024 * 1024),
+    )(*early)
+    same, limits = pl.pallas_call(
+        functools.partial(fields_kernel, (tiles, entries)),
+        name="fields",
         out_shape=(
-            state,
-            state,
-            state,
-            state,
-            jax.ShapeDtypeStruct((bands * entries * vrows // 2, LANES), F32),
             jax.ShapeDtypeStruct((COLORS * MOST, 2 * LANES, 2 * LANES), BF16),
             jax.ShapeDtypeStruct((3, COLORS), I32),
         ),
-        in_specs=[vmem()] * 4,
-        out_specs=(vmem(),) * 6 + (smem(),),
-        scratch_shapes=[square, square],
+        in_specs=[vmem()] * 2,
+        out_specs=(vmem(), smem()),
+        scratch_shapes=[square, square] + [pltpu.VMEM((2 * groups, LANES), F32)] * 2,
         compiler_params=pltpu.CompilerParams(vmem_limit_bytes=20 * 1024 * 1024),
-    )(*early)
+    )(early[0], early[2])
     keep = pl.pallas_call(
         functools.partial(side_kernel, (bands, fields, stars)),
         name="side",
@@ -636,7 +661,7 @@
             pltpu.VMEM((fields // LANES, LANES), F32),
         ],
         compiler_params=pltpu.CompilerParams(vmem_limit_bytes=20 * 1024 * 1024),
-    )(limits, *late, *ready, keep)
+    )(limits, *late, *ready, same, keep)
 
     misfit = sky_sum(partial, bands, tiles)[0, :SWEEPS] / (obs * stars * tiles)
     return zp, means, misfit[:, None]

time: 100 us -> 101 us (1.010)
    pallas_call x0 -> x1, Pallas kernels: none -> 3.44 us  [local_body(): pl.pallas_call(functools.partial(fields_kernel, (tiles, entries)), name='...]
    pallas_call x1, Pallas kernels: 7.1 us -> 3.84 us  [local_body(): pl.pallas_call(functools.partial(ready_kernel, (tiles, bands, entries)),...]
where the time goes in v2:
time: 101 us
  Pallas kernels  36.7 us (36%)
  waiting for transfers between devices  27.1 us (27%)
  starting transfers between devices  20.4 us (20%)
  blocking collectives  10.4 us (10%)
  local copies, waits for them, and re-layouts  2.98 us (3%)
  other arithmetic  2.35 us (2%)
    ppermute x17, waiting for transfers between devices, move(): return lax.ppermute(value, ('sky', 'band'), pairs)  27.1 us
    pallas_call x1, Pallas kernels, local_body(): pl.pallas_call(functools.partial(sweep_kernel, (tiles, bands, obs, stars,...  21.1 us
    ppermute x17, starting transfers between devices, move(): return lax.ppermute(value, ('sky', 'band'), pairs)  20.4 us
    all_gather x1, blocking collectives, local_body(): raw = lax.all_gather(packed, 'band', axis=0)  10.4 us
    pallas_call x1, Pallas kernels, local_body(): pl.pallas_call(functools.partial(tile_kernel, (bands, obs, stars, blocks,...  4.56 us
    pallas_call x1, Pallas kernels, local_body(): pl.pallas_call(functools.partial(ready_kernel, (tiles, bands, entries)),...  3.84 us
    pallas_call x1, Pallas kernels, local_body(): pl.pallas_call(functools.partial(fields_kernel, (tiles, entries)), name='...  3.44 us
    unnamed x10, local copies, waits for them, and re-layouts  2.94 us
  transfers between devices with their start and end apart: 17, of which 7 were waited for; matrix products, arithmetic and copies ran while one was open for 4% of the time, Pallas kernels for 9%

profile of v2, /device:TPU:0, one launch (start us, length us, event | category | flops | bytes accessed | tf_op | source)
XLA Modules:
  0.0 100.6 jit_solution(9187727566402662518)
XLA Ops:
  0.6 1.6 %pack.1 = f32[16,2176]{1,0:T(8,128)} custom-call(f32[8,2048]{1,0:T(8,128)} %bitcast.26, f32[8,2048]{1,0:T(8,128)} %bitcast.37, s32[8,2048]{1,0:T(8,128)} %bitcast.38), custom_call_target="tpu_custom_call" | custom-call | tf_op jit(solution)/shard_map/pack/pallas_call | solution.py:571
  2.2 10.4 %all-gather = f32[64,2176]{1,0:T(8,128)} all-gather(f32[16,2176]{1,0:T(8,128)} %pack.1), channel_id=2, replica_groups=mesh['sky'=8,'band'=4] {'band'}, dimensions={0}, use_global_device_ids=true | all-gather | bytes 696320 | tf_op jit(solution)/shard_map/all_gather | solution.py:578
  12.6 4.6 %tile.1 = (f32[136,128]{1,0:T(8,128)}, f32[144,128]{1,0:T(8,128)}, s32[8,128]{1,0:T(8,128)}) custom-call(f32[4,4]{1,0:T(4,128)} %terms_ref.3, f32[4,16,2176]{2,1,0:T(8,128)} %bitcast.24, f32[8,2048]{1,0:T(8,128)} %bitcast.27, s32[8,32]{1,0:T(8,128)} %lists_ref.1, s32[32,128]{1,0:T(8,128)} %bitcast.40), custom_call_target="tpu_custom_call" | custom-call | tf_op jit(solution)/shard_map/tile/pallas_call | solution.py:581
  17.2 1.6 %collective-permute-start = (f32[136,128]{1,0:T(8,128)}, f32[136,128]{1,0:T(8,128)S(1)}, u32[]{:S(2)}, u32[]{:S(2)}) collective-permute-start(f32[136,128]{1,0:T(8,128)} %get-tuple-element.16), channel_id=1, source_target_pairs={{0,8},{1,9},{2,10},{3,11},{4,12},{5,13},{6,14},{7,15},{8,16},{9,17... | collective-permute-start | bytes 208904 | tf_op jit(solution)/shard_map/ppermute | solution.py:534
  18.7 2.6 %collective-permute-start.1 = (f32[136,128]{1,0:T(8,128)}, f32[136,128]{1,0:T(8,128)S(1)}, u32[]{:S(2)}, u32[]{:S(2)}) collective-permute-start(f32[136,128]{1,0:T(8,128)} %get-tuple-element.16), channel_id=1, source_target_pairs={{0,16},{1,17},{2,18},{3,19},{4,20},{5,21},{6,22},{7,23},{8,24},{9,... | collective-permute-start | bytes 208904 | tf_op jit(solution)/shard_map/ppermute | solution.py:534
  21.3 1.3 %collective-permute-start.2 = (f32[136,128]{1,0:T(8,128)}, f32[136,128]{1,0:T(8,128)S(1)}, u32[]{:S(2)}, u32[]{:S(2)}) collective-permute-start(f32[136,128]{1,0:T(8,128)} %get-tuple-element.16), channel_id=1, source_target_pairs={{0,24},{1,25},{2,26},{3,27},{4,28},{5,29},{6,30},{7,31},{8,0},{9,1... | collective-permute-start | bytes 208904 | tf_op jit(solution)/shard_map/ppermute | solution.py:534
  22.7 0.7 collective-permute-start.5
  23.7 0.9 constant_dynamic-update-slice_fusion.9
  24.6 0.9 constant_dynamic-update-slice_fusion.4
  25.5 2.9 %collective-permute-start.7 = (f32[144,128]{1,0:T(8,128)}, f32[144,128]{1,0:T(8,128)S(1)}, u32[]{:S(2)}, u32[]{:S(2)}) collective-permute-start(f32[144,128]{1,0:T(8,128)} %get-tuple-element.18), channel_id=1, source_target_pairs={{0,24},{1,25},{2,26},{3,27},{4,28},{5,29},{6,30},{7,31},{8,0},{9,1... | collective-permute-start | bytes 221192 | tf_op jit(solution)/shard_map/ppermute | solution.py:534
  28.4 0.9 pad_maximum_fusion.1
  29.3 1.6 %collective-permute-start.3 = (f32[4,136,128]{2,1,0:T(8,128)S(1)}, f32[4,136,128]{2,1,0:T(8,128)S(1)}, u32[]{:S(2)}, u32[]{:S(2)}) collective-permute-start(f32[4,136,128]{2,1,0:T(8,128)S(1)} %pad_maximum_fusion.1), channel_id=1, source_target_pairs={{0,4},{1,3},{2,6},{3,1},{4,0},{5,7},{6,2},{7,5},{8,12},{9,11},{10,... | collective-permute-start | bytes 835592 | tf_op jit(solution)/shard_map/ppermute | solution.py:534
  30.9 2.1 %collective-permute-done.6 = f32[144,128]{1,0:T(8,128)S(1)} collective-permute-done((f32[144,128]{1,0:T(8,128)}, f32[144,128]{1,0:T(8,128)S(1)}, u32[]{:S(2)}, u32[]{:S(2)}) %collective-permute-start.6) | collective-permute-done | bytes 73760 | tf_op jit(solution)/shard_map/ppermute | solution.py:534
  33.0 0.9 pad_maximum_fusion
  34.0 1.6 %collective-permute-start.8 = (f32[4,144,128]{2,1,0:T(8,128)S(1)}, f32[4,144,128]{2,1,0:T(8,128)S(1)}, u32[]{:S(2)}, u32[]{:S(2)}) collective-permute-start(f32[4,144,128]{2,1,0:T(8,128)S(1)} %pad_maximum_fusion), channel_id=1, source_target_pairs={{0,4},{1,3},{2,6},{3,1},{4,0},{5,7},{6,2},{7,5},{8,12},{9,11},{10,... | collective-permute-start | bytes 884744 | tf_op jit(solution)/shard_map/ppermute | solution.py:534
  35.6 5.2 %collective-permute-done.8 = f32[4,144,128]{2,1,0:T(8,128)S(1)} collective-permute-done((f32[4,144,128]{2,1,0:T(8,128)S(1)}, f32[4,144,128]{2,1,0:T(8,128)S(1)}, u32[]{:S(2)}, u32[]{:S(2)}) %collective-permute-start.8) | collective-permute-done | bytes 294944 | tf_op jit(solution)/shard_map/ppermute | solution.py:534
  40.8 0.6 collective-permute-start.9
  41.4 1.5 %collective-permute-start.12 = (f32[8,136,128]{2,1,0:T(8,128)S(1)}, f32[8,136,128]{2,1,0:T(8,128)}, u32[]{:S(2)}, u32[]{:S(2)}) collective-permute-start(f32[8,136,128]{2,1,0:T(8,128)S(1)} %constant_dynamic-update-slice_fusion.near_ref), channel_id=1, source_target_pairs={{0,2},{1,5},{2,0},{3,7},{4,6},{5,1},{6,4},{7,3},{8,10},{9,13},{10,... | collective-permute-start | bytes 1671176 | tf_op jit(solution)/shard_map/ppermute | solution.py:534
  43.0 7.8 %collective-permute-done.9.across_ref = f32[8,144,128]{2,1,0:T(8,128)S(1)} collective-permute-done((f32[8,144,128]{2,1,0:T(8,128)S(1)}, f32[8,144,128]{2,1,0:T(8,128)S(1)}, u32[]{:S(2)}, u32[]{:S(2)}) %collective-permute-start.9) | collective-permute-done | bytes 589856 | tf_op jit(solution)/shard_map/ppermute | solution.py:534
  51.2 5.6 %collective-permute-done.12.across_ref = f32[8,136,128]{2,1,0:T(8,128)} collective-permute-done((f32[8,136,128]{2,1,0:T(8,128)S(1)}, f32[8,136,128]{2,1,0:T(8,128)}, u32[]{:S(2)}, u32[]{:S(2)}) %collective-permute-start.12) | collective-permute-done | bytes 557088 | tf_op jit(solution)/shard_map/ppermute | solution.py:534
  56.8 2.2 %side.1.keep_ref = f32[80,2176]{1,0:T(8,128)} custom-call(f32[4,4]{1,0:T(4,128)} %terms_ref.3, s32[32,128]{1,0:T(8,128)} %bitcast.39, f32[4,16,2176]{2,1,0:T(8,128)} %bitcast.25, f32[8,2048]{1,0:T(8,128)} %bitcast.28, s32[8,128]{1,0:T(8,128)} %get-tuple-element.25.tab_in), custom_call_target="tpu_custom_call" | custom-call | tf_op jit(solution)/shard_map/side/pallas_call | solution.py:628
  59.0 3.4 %fields.1 = (bf16[72,256,256]{2,1,0:T(8,128)(2,1)S(1)}, s32[3,8]{1,0:T(4,128)S(1)}) custom-call(f32[8,136,128]{2,1,0:T(8,128)S(1)} %constant_dynamic-update-slice_fusion.near_ref, f32[8,136,128]{2,1,0:T(8,128)S(1)} %collective-permute-done.4.far_near_ref), custom_call_target="tpu_custom_call" | custom-call | tf_op jit(solution)/shard_map/fields/pallas_call | solution.py:616
  62.4 3.8 %ready.1 = (f32[64,128]{1,0:T(8,128)S(1)}, f32[64,128]{1,0:T(8,128)S(1)}, f32[64,128]{1,0:T(8,128)S(1)}, f32[64,128]{1,0:T(8,128)S(1)}, f32[4096,128]{1,0:T(8,128)S(1)}) custom-call(f32[8,136,128]{2,1,0:T(8,128)S(1)} %constant_dynamic-update-slice_fusion.near_ref, f32[8,136,128]{2,1,0:T(8,128)} %collective-permute-done.12.across_ref, ...), custom_call_target="tpu_custom_call" | custom-call | tf_op jit(solution)/shard_map/ready/pallas_call | solution.py:607
  66.3 1.1 %copy-done = f32[80,2176]{1,0:T(8,128)S(1)} copy-done((f32[80,2176]{1,0:T(8,128)S(1)}, f32[80,2176]{1,0:T(8,128)}, u32[]{:S(2)}) %copy-start) | copy-done | bytes 696344
  67.4 21.1 %sweeps.1 = (f32[1,512]{1,0:T(1,128)}, f32[1,2048]{1,0:T(1,128)}, f32[1,128]{1,0:T(1,128)S(1)}) custom-call(s32[3,8]{1,0:T(4,128)S(1)} %get-tuple-element.17.lim_ref, f32[8,144,128]{2,1,0:T(8,128)S(1)} %constant_dynamic-update-slice_fusion.5.near_ref, f32[8,144,128]{2,1,0:T(8,128)S(1)} %collective-permute-done.9.across_ref, ...), custom_call_target="tpu_custom_call" | custom-call | tf_op jit(solution)/shard_map/sweeps/pallas_call | solution.py:636
  88.5 1.5 %collective-permute-start.14 = (f32[1,128]{1,0:T(1,128)S(1)}, f32[1,128]{1,0:T(1,128)S(1)}, u32[]{:S(2)}, u32[]{:S(2)}) collective-permute-start(f32[1,128]{1,0:T(1,128)S(1)} %get-tuple-element.28), channel_id=1, source_target_pairs={{0,4},{1,5},{2,6},{3,7},{4,0},{5,1},{6,2},{7,3},{8,12},{9,13},{10,... | collective-permute-start | bytes 1544 | tf_op jit(solution)/shard_map/ppermute | solution.py:534
  90.0 2.0 %collective-permute-done.14 = f32[1,128]{1,0:T(1,128)S(1)} collective-permute-done((f32[1,128]{1,0:T(1,128)S(1)}, f32[1,128]{1,0:T(1,128)S(1)}, u32[]{:S(2)}, u32[]{:S(2)}) %collective-permute-start.14) | collective-permute-done | bytes 544 | tf_op jit(solution)/shard_map/ppermute | solution.py:534
  92.1 2.0 %collective-permute-start.15 = (f32[1,128]{1,0:T(1,128)S(1)}, f32[1,128]{1,0:T(1,128)S(1)}, u32[]{:S(2)}, u32[]{:S(2)}) collective-permute-start(f32[1,128]{1,0:T(1,128)S(1)} %add.9), channel_id=1, source_target_pairs={{0,8},{1,9},{2,10},{3,11},{4,12},{5,13},{6,14},{7,15},{8,0},{9,1},... | collective-permute-start | bytes 1544 | tf_op jit(solution)/shard_map/ppermute | solution.py:534
  94.1 1.6 %collective-permute-done.15 = f32[1,128]{1,0:T(1,128)S(1)} collective-permute-done((f32[1,128]{1,0:T(1,128)S(1)}, f32[1,128]{1,0:T(1,128)S(1)}, u32[]{:S(2)}, u32[]{:S(2)}) %collective-permute-start.15) | collective-permute-done | bytes 544 | tf_op jit(solution)/shard_map/ppermute | solution.py:534
  95.6 1.6 %collective-permute-start.16 = (f32[1,128]{1,0:T(1,128)S(1)}, f32[1,128]{1,0:T(1,128)S(1)}, u32[]{:S(2)}, u32[]{:S(2)}) collective-permute-start(f32[1,128]{1,0:T(1,128)S(1)} %add.10), channel_id=1, source_target_pairs={{0,16},{1,17},{2,18},{3,19},{4,20},{5,21},{6,22},{7,23},{8,24},{9,... | collective-permute-start | bytes 1544 | tf_op jit(solution)/shard_map/ppermute | solution.py:534
  97.2 2.9 %collective-permute-done.16 = f32[1,128]{1,0:T(1,128)S(1)} collective-permute-done((f32[1,128]{1,0:T(1,128)S(1)}, f32[1,128]{1,0:T(1,128)S(1)}, u32[]{:S(2)}, u32[]{:S(2)}) %collective-permute-start.16) | collective-permute-done | bytes 544 | tf_op jit(solution)/shard_map/ppermute | solution.py:534
  100.1 0.5 multiply_bitcast_fusion
  (27 shorter events, 1.0 us)
Async XLA Ops:
  17.2 8.3 %collective-permute-start = (f32[136,128]{1,0:T(8,128)}, f32[136,128]{1,0:T(8,128)S(1)}, u32[]{:S(2)}, u32[]{:S(2)}) collective-permute-start(f32[136,128]{1,0:T(8,128)} %get-tuple-element.16), channel_id=1, source_target_pairs={{0,8},{1,9},{2,10},{3,11},{4,12},{5,13},{6,14},{7,15},{8,16},{9,17... | collective-permute-start | bytes 208904 | tf_op jit(solution)/shard_map/ppermute | solution.py:534
  18.7 9.7 %collective-permute-start.1 = (f32[136,128]{1,0:T(8,128)}, f32[136,128]{1,0:T(8,128)S(1)}, u32[]{:S(2)}, u32[]{:S(2)}) collective-permute-start(f32[136,128]{1,0:T(8,128)} %get-tuple-element.16), channel_id=1, source_target_pairs={{0,16},{1,17},{2,18},{3,19},{4,20},{5,21},{6,22},{7,23},{8,24},{9,... | collective-permute-start | bytes 208904 | tf_op jit(solution)/shard_map/ppermute | solution.py:534
  21.3 7.1 %collective-permute-start.2 = (f32[136,128]{1,0:T(8,128)}, f32[136,128]{1,0:T(8,128)S(1)}, u32[]{:S(2)}, u32[]{:S(2)}) collective-permute-start(f32[136,128]{1,0:T(8,128)} %get-tuple-element.16), channel_id=1, source_target_pairs={{0,24},{1,25},{2,26},{3,27},{4,28},{5,29},{6,30},{7,31},{8,0},{9,1... | collective-permute-start | bytes 208904 | tf_op jit(solution)/shard_map/ppermute | solution.py:534
  22.7 8.3 %collective-permute-start.5 = (f32[144,128]{1,0:T(8,128)}, f32[144,128]{1,0:T(8,128)S(1)}, u32[]{:S(2)}, u32[]{:S(2)}) collective-permute-start(f32[144,128]{1,0:T(8,128)} %get-tuple-element.18), channel_id=1, source_target_pairs={{0,8},{1,9},{2,10},{3,11},{4,12},{5,13},{6,14},{7,15},{8,16},{9,17... | collective-permute-start | bytes 221192 | tf_op jit(solution)/shard_map/ppermute | solution.py:534
  23.4 9.6 %collective-permute-start.6 = (f32[144,128]{1,0:T(8,128)}, f32[144,128]{1,0:T(8,128)S(1)}, u32[]{:S(2)}, u32[]{:S(2)}) collective-permute-start(f32[144,128]{1,0:T(8,128)} %get-tuple-element.18), channel_id=1, source_target_pairs={{0,16},{1,17},{2,18},{3,19},{4,20},{5,21},{6,22},{7,23},{8,24},{9,... | collective-permute-start | bytes 221192 | tf_op jit(solution)/shard_map/ppermute | solution.py:534
  25.5 7.5 %collective-permute-start.7 = (f32[144,128]{1,0:T(8,128)}, f32[144,128]{1,0:T(8,128)S(1)}, u32[]{:S(2)}, u32[]{:S(2)}) collective-permute-start(f32[144,128]{1,0:T(8,128)} %get-tuple-element.18), channel_id=1, source_target_pairs={{0,24},{1,25},{2,26},{3,27},{4,28},{5,29},{6,30},{7,31},{8,0},{9,1... | collective-permute-start | bytes 221192 | tf_op jit(solution)/shard_map/ppermute | solution.py:534
  29.3 12.1 %collective-permute-start.3 = (f32[4,136,128]{2,1,0:T(8,128)S(1)}, f32[4,136,128]{2,1,0:T(8,128)S(1)}, u32[]{:S(2)}, u32[]{:S(2)}) collective-permute-start(f32[4,136,128]{2,1,0:T(8,128)S(1)} %pad_maximum_fusion.1), channel_id=1, source_target_pairs={{0,4},{1,3},{2,6},{3,1},{4,0},{5,7},{6,2},{7,5},{8,12},{9,11},{10,... | collective-permute-start | bytes 835592 | tf_op jit(solution)/shard_map/ppermute | solution.py:534
  34.0 6.8 %collective-permute-start.8 = (f32[4,144,128]{2,1,0:T(8,128)S(1)}, f32[4,144,128]{2,1,0:T(8,128)S(1)}, u32[]{:S(2)}, u32[]{:S(2)}) collective-permute-start(f32[4,144,128]{2,1,0:T(8,128)S(1)} %pad_maximum_fusion), channel_id=1, source_target_pairs={{0,4},{1,3},{2,6},{3,1},{4,0},{5,7},{6,2},{7,5},{8,12},{9,11},{10,... | collective-permute-start | bytes 884744 | tf_op jit(solution)/shard_map/ppermute | solution.py:534
  40.8 9.9 %collective-permute-start.9 = (f32[8,144,128]{2,1,0:T(8,128)S(1)}, f32[8,144,128]{2,1,0:T(8,128)S(1)}, u32[]{:S(2)}, u32[]{:S(2)}) collective-permute-start(f32[8,144,128]{2,1,0:T(8,128)S(1)} %constant_dynamic-update-slice_fusion.5.near_ref), channel_id=1, source_target_pairs={{0,2},{1,5},{2,0},{3,7},{4,6},{5,1},{6,4},{7,3},{8,10},{9,13},{10,... | collective-permute-start | bytes 1769480 | tf_op jit(solution)/shard_map/ppermute | solution.py:534
  41.4 15.4 %collective-permute-start.12 = (f32[8,136,128]{2,1,0:T(8,128)S(1)}, f32[8,136,128]{2,1,0:T(8,128)}, u32[]{:S(2)}, u32[]{:S(2)}) collective-permute-start(f32[8,136,128]{2,1,0:T(8,128)S(1)} %constant_dynamic-update-slice_fusion.near_ref), channel_id=1, source_target_pairs={{0,2},{1,5},{2,0},{3,7},{4,6},{5,1},{6,4},{7,3},{8,10},{9,13},{10,... | collective-permute-start | bytes 1671176 | tf_op jit(solution)/shard_map/ppermute | solution.py:534
  43.0 23.3 %collective-permute-start.10 = (f32[8,144,128]{2,1,0:T(8,128)S(1)}, f32[8,144,128]{2,1,0:T(8,128)S(1)}, u32[]{:S(2)}, u32[]{:S(2)}) collective-permute-start(f32[8,144,128]{2,1,0:T(8,128)S(1)} %constant_dynamic-update-slice_fusion.5.near_ref), channel_id=1, source_target_pairs={{0,1},{1,0},{2,3},{3,2},{4,5},{5,4},{6,7},{7,6},{8,9},{9,8},{10,11... | collective-permute-start | bytes 1769480 | tf_op jit(solution)/shard_map/ppermute | solution.py:534
  50.7 15.6 %collective-permute-start.11 = (f32[8,144,128]{2,1,0:T(8,128)S(1)}, f32[8,144,128]{2,1,0:T(8,128)S(1)}, u32[]{:S(2)}, u32[]{:S(2)}) collective-permute-start(f32[8,144,128]{2,1,0:T(8,128)S(1)} %collective-permute-done.9.across_ref), channel_id=1, source_target_pairs={{0,1},{1,0},{2,3},{3,2},{4,5},{5,4},{6,7},{7,6},{8,9},{9,8},{10,11... | collective-permute-start | bytes 1769480 | tf_op jit(solution)/shard_map/ppermute | solution.py:534
  50.7 8.2 %collective-permute-start.4 = (f32[8,136,128]{2,1,0:T(8,128)S(1)}, f32[8,136,128]{2,1,0:T(8,128)S(1)}, u32[]{:S(2)}, u32[]{:S(2)}) collective-permute-start(f32[8,136,128]{2,1,0:T(8,128)S(1)} %constant_dynamic-update-slice_fusion.near_ref), channel_id=1, source_target_pairs={{0,1},{1,0},{2,3},{3,2},{4,5},{5,4},{6,7},{7,6},{8,9},{9,8},{10,11... | collective-permute-start | bytes 1671176 | tf_op jit(solution)/shard_map/ppermute | solution.py:534
  56.8 5.6 %collective-permute-start.13 = (f32[8,136,128]{2,1,0:T(8,128)}, f32[8,136,128]{2,1,0:T(8,128)}, u32[]{:S(2)}, u32[]{:S(2)}) collective-permute-start(f32[8,136,128]{2,1,0:T(8,128)} %collective-permute-done.12.across_ref), channel_id=1, source_target_pairs={{0,1},{1,0},{2,3},{3,2},{4,5},{5,4},{6,7},{7,6},{8,9},{9,8},{10,11... | collective-permute-start | bytes 1671176 | tf_op jit(solution)/shard_map/ppermute | solution.py:534
  66.3 1.1 %copy-start = (f32[80,2176]{1,0:T(8,128)S(1)}, f32[80,2176]{1,0:T(8,128)}, u32[]{:S(2)}) copy-start(f32[80,2176]{1,0:T(8,128)} %side.1.keep_ref) | copy-start | bytes 2088964
  88.5 3.6 %collective-permute-start.14 = (f32[1,128]{1,0:T(1,128)S(1)}, f32[1,128]{1,0:T(1,128)S(1)}, u32[]{:S(2)}, u32[]{:S(2)}) collective-permute-start(f32[1,128]{1,0:T(1,128)S(1)} %get-tuple-element.28), channel_id=1, source_target_pairs={{0,4},{1,5},{2,6},{3,7},{4,0},{5,1},{6,2},{7,3},{8,12},{9,13},{10,... | collective-permute-start | bytes 1544 | tf_op jit(solution)/shard_map/ppermute | solution.py:534
  92.1 3.6 %collective-permute-start.15 = (f32[1,128]{1,0:T(1,128)S(1)}, f32[1,128]{1,0:T(1,128)S(1)}, u32[]{:S(2)}, u32[]{:S(2)}) collective-permute-start(f32[1,128]{1,0:T(1,128)S(1)} %add.9), channel_id=1, source_target_pairs={{0,8},{1,9},{2,10},{3,11},{4,12},{5,13},{6,14},{7,15},{8,0},{9,1},... | collective-permute-start | bytes 1544 | tf_op jit(solution)/shard_map/ppermute | solution.py:534
  95.6 4.5 %collective-permute-start.16 = (f32[1,128]{1,0:T(1,128)S(1)}, f32[1,128]{1,0:T(1,128)S(1)}, u32[]{:S(2)}, u32[]{:S(2)}) collective-permute-start(f32[1,128]{1,0:T(1,128)S(1)} %add.10), channel_id=1, source_target_pairs={{0,16},{1,17},{2,18},{3,19},{4,20},{5,21},{6,22},{7,23},{8,24},{9,... | collective-permute-start | bytes 1544 | tf_op jit(solution)/shard_map/ppermute | solution.py:534
